TPU v7x, 32 devices: a whole 2x2x4 slice. The times are simulated.
32 devices in a mesh: groups: 2 (over y), slab: 4 (over z), pencil: 2 (over x), comp: 2 (over core).
Axes of the slice: x: 2, y: 2, z: 4, core: 2. Of those that a mesh axis runs over, the one named last changes fastest.
Arguments:
- u_start: float32 [3, 64, 64, 512], P(None, ('groups', 'slab'), 'pencil', 'comp'), parts along dimension 1, may hold values from -6 to 6
- toughness: float32 [64, 64, 512], P(('groups', 'slab'), 'pencil', 'comp'), parts along dimension 0, may hold values from 0.3 to 1.5
- crack_label: int32 [64, 64, 512], P(('groups', 'slab'), 'pencil', 'comp'), parts along dimension 0, may hold values from 0 to 2
- obs_weight: bfloat16 [32, 64, 2, 4096], P('slab', 'pencil', 'comp'), may hold values from -0.75 to 0.75
- sensor_cell: int32 [4096], replicated, may hold values from 0 to 4095
Outputs:
- moved: float32 [3, 64, 64, 512], P(None, ('groups', 'slab'), 'pencil', 'comp'), parts along dimension 1
- damage: float32 [64, 64, 512], P(('groups', 'slab'), 'pencil', 'comp'), parts along dimension 0
- readings: float32 [3, 8192], P(None, 'groups'), parts along dimension 1
There are 2 independent parts, one for each index of `groups`. A program takes and returns all parts, laid end to end along the dimension named above; an argument that names none is the same for every part. Nothing has to cross between parts.
Inputs may be any that keep to these rules, and one draw needn't show every extreme that they name: `sensor_cell`: numbers cell blocks as (64 z + y) * 2 + h. `crack_label`: 0 intact, 1 partly cracked, 2 cracked.
All inputs are finite; a program needn't handle non-finite values.
Results may differ from a plain program's by a relative error of at most 0.003.
Values sent between devices are 32-bit elements; how exact they have to be, the bound alone decides.
A program may use at most 128 MiB of HBM per device.

v0:
```python
import itertools

import jax
import jax.numpy as jnp
import numpy as np
from jax import lax
from jax.experimental import pallas as pl
from jax.experimental.pallas import tpu as pltpu
from jax.sharding import PartitionSpec as P

RESIDUAL_STIFF = 0.001
TIME_DISP = 0.15
TIME_DAMAGE = 0.08
DAMAGE_LEVEL = 0.45
POINT_GAIN = 8.0
AXES = ("slab", "pencil", "comp")
MESH = pl.DeviceIdType.MESH
F32 = jnp.float32


def third_angle_poly():
    nodes = 0.5 + 0.5 * np.cos(np.pi * (np.arange(200) + 0.5) / 200)
    fit = np.polynomial.chebyshev.Chebyshev.fit(
        nodes, np.cos(np.arccos(nodes) / 3.0), 8, domain=[0.0, 1.0]
    )
    return [float(c) for c in fit.convert(kind=np.polynomial.Polynomial).coef]


POLY = third_angle_poly()

DIRECTIONS = [
    d for d in itertools.product((-1, 0, 1), repeat=3) if 1 <= sum(map(abs, d)) <= 2
]
FAST_X = [d for d in DIRECTIONS if d[0] == 0 and d[1] == 0]
FAST_Y = [d for d in DIRECTIONS if d[0] == 0 and d[1] != 0]
FACES = [(0, 0, -1), (0, 0, 1), (-1, 0, 0), (1, 0, 0), (0, -1, 0), (0, 1, 0)]
ORDER = FACES + [d for d in FAST_Y if d[2]] + [d for d in DIRECTIONS if d[0] and (d[1] or d[2])]
SLOW = [d for d in DIRECTIONS if d[0] != 0]


def energy_of(e00, e11, e22, e01, e02, e12):
    trace = e00 + e11 + e22
    mean = trace * (1.0 / 3.0)
    d0, d1, d2 = e00 - mean, e11 - mean, e22 - mean
    p2 = (d0 * d0 + d1 * d1 + d2 * d2) * (1.0 / 6.0) + (
        e01 * e01 + e02 * e02 + e12 * e12
    ) * (1.0 / 3.0)
    inv = lax.rsqrt(jnp.maximum(p2, 1e-36))
    p = p2 * inv
    b0, b1, b2 = d0 * inv, d1 * inv, d2 * inv
    b01, b02, b12 = e01 * inv, e02 * inv, e12 * inv
    half_det = 0.5 * (
        b0 * (b1 * b2 - b12 * b12)
        - b01 * (b01 * b2 - b12 * b02)
        + b02 * (b01 * b12 - b1 * b02)
    )
    r = jnp.minimum(jnp.abs(half_det), 1.0)
    c = jnp.full_like(r, POLY[-1])
    for coefficient in POLY[-2::-1]:
        c = c * r + coefficient
    tc = p * c
    t = jnp.where(half_det < 0.0, -tc, tc)
    s2 = jnp.maximum(1.0 - c * c, 0.0)
    delta = p * (s2 * lax.rsqrt(jnp.maximum(s2, 1e-30))) * float(np.sqrt(3.0))
    f1 = jnp.maximum(mean + 2.0 * t, 0.0)
    f2 = jnp.maximum(mean - t + delta, 0.0)
    f3 = jnp.maximum(mean - t - delta, 0.0)
    ft = jnp.maximum(trace, 0.0)
    return 0.75 * ft * ft + f1 * f1 + f2 * f2 + f3 * f3


def make_kernel(planes, rows, columns, sensors, sizes, owners):
    n_slab, n_pencil, n_comp = sizes
    count = n_slab * n_pencil * n_comp
    Z, R, C = planes, rows, columns
    piece = sensors // owners
    half = piece // 2

    def kernel(u_hbm, tough_hbm, crack_hbm, weight_hbm, cell_ref,
               moved_ref, damage_ref, read_ref,
               U, XR, YR, YP, YXR, TZ, tough, crack, weight, pooled_t, hot, partial, RB, GB,
               in_sem, send_sem, recv_sem, rs_send, rs_recv, ag_send, ag_recv):
        me = [lax.axis_index(a) for a in AXES]
        flat = (me[0] * n_pencil + me[1]) * n_comp + me[2]

        def device(index):
            return {
                "slab": index // (n_pencil * n_comp),
                "pencil": (index // n_comp) % n_pencil,
                "comp": index % n_comp,
            }

        loads = [
            pltpu.make_async_copy(u_hbm, U.at[0, 0:3, 2:Z + 2, 0:R, 0:C], in_sem.at[0]),
            pltpu.make_async_copy(crack_hbm, crack, in_sem.at[1]),
            pltpu.make_async_copy(tough_hbm, tough, in_sem.at[2]),
            pltpu.make_async_copy(weight_hbm, weight, in_sem.at[3]),
        ]
        for load in loads:
            load.start()

        for step in range(2):
            for z in (0, 1, Z + 2, Z + 3):
                U[step, :, z, 0:R, 0:C] = jnp.zeros((4, R, C), F32)
        XR[...] = jnp.zeros(XR.shape, F32)
        YR[...] = jnp.zeros(YR.shape, F32)
        YXR[...] = jnp.zeros(YXR.shape, F32)

        barrier = pltpu.get_barrier_semaphore()

        def greet(k, carry):
            pl.semaphore_signal(
                barrier, inc=1, device_id=device((flat + k) % count), device_id_type=MESH
            )
            return carry

        lax.fori_loop(1, count, greet, 0)
        pl.semaphore_wait(barrier, count - 1)

        loads[1].wait()

        def label(z, carry):
            U[0, 3, z + 2, 0:R, 0:C] = DAMAGE_LEVEL * crack[z].astype(F32)
            return carry

        lax.fori_loop(0, Z, label, 0)
        loads[0].wait()

        def copies(step, d):
            dz, dy, dx = d
            sy, sx = (dy + 1) // 2, (dx + 1) // 2
            lanes = slice(C - 128, C) if dx > 0 else slice(0, 128)
            edge = Z - 1 if dz > 0 else 0
            halo = 0 if dz > 0 else Z + 1
            if dz and not dy and not dx:
                first = Z if dz > 0 else 2
                target = 0 if dz > 0 else Z + 2
                pairs = [
                    (U.at[step, 0:3, first:first + 2, 0:R, 0:C],
                     U.at[step, 0:3, target:target + 2, 0:R, 0:C]),
                    (U.at[step, 3, edge + 2, 0:R, 0:C], U.at[step, 3, halo + 1, 0:R, 0:C]),
                ]
            elif dz and dy:
                pairs = [(YP.at[step, sy, edge], YR.at[step, 1 - sy, halo])]
            elif dz and dx:
                pairs = [(U.at[step, 0:3, edge + 2, 0:R, lanes], XR.at[step, 1 - sx, 0:3, halo])]
            elif dy and dx:
                pairs = [(YP.at[step, sy, :, :, lanes], YXR.at[step, 1 - sy, 1 - sx])]
            elif dy:
                pairs = [(YP.at[step, sy], YR.at[step, 1 - sy, 1:Z + 1])]
            else:
                pairs = [(U.at[step, :, 2:Z + 2, 0:R, lanes], XR.at[step, 1 - sx, :, 1:Z + 1])]
            index = DIRECTIONS.index(d)
            return [
                pltpu.make_async_remote_copy(
                    src_ref=src,
                    dst_ref=dst,
                    send_sem=send_sem.at[step, index, k],
                    recv_sem=recv_sem.at[step, index, k],
                    device_id={a: m + o for a, m, o in zip(AXES, me, d)},
                    device_id_type=MESH,
                )
                for k, (src, dst) in enumerate(pairs)
            ]

        def inside(d, sign):
            ok = None
            for m, o, n in zip(me, d, sizes):
                if o:
                    here = m + 1 < n if sign * o > 0 else m >= 1
                    ok = here if ok is None else jnp.logical_and(ok, here)
            return ok

        def feasible(d):
            return all(n > 1 for o, n in zip(d, sizes) if o)

        def each(step, directions, sign, action):
            for d in directions:
                if feasible(d):
                    @pl.when(inside(d, sign))
                    def _():
                        for copy in copies(step, d):
                            action(copy)

        row8 = lax.broadcasted_iota(jnp.int32, (8, C), 0)
        row8t = lax.broadcasted_iota(jnp.int32, (8, 128), 0)
        lane8 = lax.broadcasted_iota(jnp.int32, (8, 128), 1)
        lane_r = lax.broadcasted_iota(jnp.int32, (R, 128), 1)

        def roll(value, shift, axis):
            shift = shift % value.shape[axis]
            return pltpu.roll(value, shift, axis) if shift else value

        def pack(step):
            def one(z, carry):
                low = [U[step, f, z + 2, 0:8, 0:C] for f in range(4)]
                high = [U[step, f, z + 2, R - 8:R, 0:C] for f in range(4)]
                for side, tiles, shifts in (
                    (0, low, (0, 2, 4, 6)), (1, high, (2, 4, 6, 7))
                ):
                    rolled = [roll(t, s, 0) for t, s in zip(tiles, shifts)]
                    YP[step, side, z] = jnp.where(
                        row8 < 2, rolled[0],
                        jnp.where(row8 < 4, rolled[1], jnp.where(row8 < 6, rolled[2], rolled[3])),
                    )
                return carry

            lax.fori_loop(0, Z, one, 0)

        def merged(low, high, f, row):
            up, down = ((8 - 2 * f) % 8, 6 - 2 * f) if f < 3 else (2, 1)
            return jnp.where(row < 4, roll(high, up, 0), roll(low, down, 0))

        def unpack_x(step, z, fields):
            for f in range(fields):
                U[step, f, z + 2, 0:R, C:C + 128] = jnp.where(
                    lane_r < 64, XR[step, 1, f, z + 1], XR[step, 0, f, z + 1]
                )

        def unpack_y(step, z, fields):
            low, high = YR[step, 0, z + 1], YR[step, 1, z + 1]
            for f in range(fields):
                U[step, f, z + 2, R:R + 8, 0:C] = merged(low, high, f, row8)
            if fields == 4:
                left, right = [
                    [YXR[step, sy, sx, z] for sy in range(2)] for sx in range(2)
                ]
                for f in range(3):
                    U[step, f, z + 2, R:R + 8, C:C + 128] = jnp.where(
                        lane8 < 64, merged(*right, f, row8t), merged(*left, f, row8t)
                    )

        def ends(step, z):
            now = [U[step, i, z + 2] for i in range(3)]
            gz = [
                U[step, i, z + 3, 0:R, 0:C] - U[step, i, z + 1, 0:R, 0:C] for i in range(3)
            ]

            def along(value, axis):
                return (roll(value, -1, axis) - roll(value, 1, axis))[0:R, 0:C]

            gy0, gy1 = along(now[0], 0), along(now[1], 0)
            gx0, gx2 = along(now[0], 1), along(now[2], 1)
            keep = 1.0 - U[step, 3, z + 2, 0:R, 0:C]
            g = (0.5 * TIME_DISP) * (keep * keep + RESIDUAL_STIFF)
            TZ[z + 1, 0] = g * (gz[0] + 0.75 * (gz[0] + gy1 + gx2))
            TZ[z + 1, 1] = g * (0.5 * (gz[1] + gy0))
            TZ[z + 1, 2] = g * (0.5 * (gz[2] + gx0))

        def store(step, f, z, value):
            if step == 0:
                U[1, f, z + 2, 0:R, 0:C] = value
            elif f < 3:
                moved_ref[f, z] = value
            else:
                damage_ref[z] = value

        def load(step, f, z):
            return U[1, f, z + 2, 0:R, 0:C] if step == 0 else moved_ref[f, z]

        def body(step, z):
            now = [U[step, i, z + 2] for i in range(3)]
            gz = [U[step, i, z + 3] - U[step, i, z + 1] for i in range(3)]
            gy = [roll(v, -1, 0) - roll(v, 1, 0) for v in now]
            gx = [roll(v, -1, 1) - roll(v, 1, 1) for v in now]
            d = U[step, 3, z + 2]
            keep = 1.0 - d
            g = (0.5 * TIME_DISP) * (keep * keep + RESIDUAL_STIFF)
            lam = 0.75 * (gz[0] + gy[1] + gx[2])
            s01 = 0.5 * (gz[1] + gy[0])
            s02 = 0.5 * (gz[2] + gx[0])
            s12 = 0.5 * (gy[2] + gx[1])
            in_y = [g * s01, g * (gy[1] + lam), g * s12]
            in_x = [(g * s02)[0:R], in_y[2][0:R], (g * (gx[2] + lam))[0:R]]
            TZ[z + 1, 0] = (g * (gz[0] + lam))[0:R, 0:C]
            TZ[z + 1, 1] = in_y[0][0:R, 0:C]
            TZ[z + 1, 2] = in_x[0][:, 0:C]
            for i in range(3):
                ty = in_y[i][:, 0:C]
                force = (roll(ty, -1, 0) - roll(ty, 1, 0))[0:R] + (
                    roll(in_x[i], -1, 1) - roll(in_x[i], 1, 1)
                )[:, 0:C]
                store(step, i, z, now[i][0:R, 0:C] + force)

            def core(value):
                return value[0:R, 0:C]

            energy = energy_of(
                0.5 * core(gz[0]), 0.5 * core(gy[1]), 0.5 * core(gx[2]),
                0.5 * core(s01), 0.5 * core(s02), 0.5 * core(s12),
            )
            dy = d[:, 0:C]
            dx = d[0:R]
            dc = core(d)
            lap = (
                U[step, 3, z + 3, 0:R, 0:C] + U[step, 3, z + 1, 0:R, 0:C]
                + (roll(dy, -1, 0) + roll(dy, 1, 0))[0:R]
                + (roll(dx, -1, 1) + roll(dx, 1, 1))[:, 0:C]
                - 6.0 * dc
            )
            store(step, 3, z, dc + TIME_DAMAGE * (
                2.0 * (1.0 - dc) * energy + tough[z] * (lap - dc)
            ))

        def finish(step, z):
            for i in range(3):
                store(step, i, z, load(step, i, z) + (TZ[z + 2, i] - TZ[z, i]))

        def loop(start, stop, function):
            def one(z, carry):
                function(z)
                return carry

            lax.fori_loop(start, stop, one, 0)

        for step in range(2):
            pack(step)
            each(step, ORDER, 1, lambda copy: copy.start())
            if step == 0:
                loads[2].wait()
                base = me[0] * Z * (R * n_pencil) + me[1] * R
                row_id = lax.broadcasted_iota(jnp.int32, (R, 512), 0) * n_comp

                def choose(z, carry):
                    start = (base + z * (R * n_pencil)) * n_comp + me[2]
                    for s in range(0, sensors, 512):
                        hit = row_id == cell_ref[:, s:s + 512] - start
                        hot[z, :, s:s + 512] = jnp.where(hit, POINT_GAIN, 0.0).astype(jnp.bfloat16)
                    return carry

                lax.fori_loop(0, Z, choose, 0)
            each(step, FAST_X, -1, lambda copy: copy.wait_recv())
            loop(0, Z, lambda z: unpack_x(step, z, 4))
            each(step, FAST_Y, -1, lambda copy: copy.wait_recv())
            loop(0, Z, lambda z: unpack_y(step, z, 4))
            loop(1, Z - 1, lambda z: body(step, z))
            each(step, SLOW, -1, lambda copy: copy.wait_recv())
            for z in (-1, Z):
                unpack_x(step, z, 3)
                unpack_y(step, z, 3)
            loop(0, 2, lambda k: body(step, k * (Z - 1)))
            loop(0, 2, lambda k: ends(step, k * (Z + 1) - 1))
            loop(0, Z, lambda z: finish(step, z))
            each(step, ORDER, 1, lambda copy: copy.wait_send())

        def pool(z):
            total = jnp.zeros((R, 128), F32)
            for i in range(3):
                mean = jnp.sum(moved_ref[i, z], axis=1, keepdims=True) * (1.0 / C)
                total = jnp.where(lane_r == i, mean, total)
            pooled_t[pl.ds(pl.multiple_of(z * R, R), R), :] = total

        loop(0, Z, pool)
        pooled = pooled_t[...].T[0:8].astype(jnp.bfloat16)
        loads[3].wait()
        def scatter(q):
            return pltpu.make_async_remote_copy(
                src_ref=partial.at[q], dst_ref=RB.at[flat],
                send_sem=rs_send.at[q], recv_sem=rs_recv.at[flat],
                device_id=device(q), device_id_type=MESH,
            )

        def scatter_from(k):
            return pltpu.make_async_remote_copy(
                src_ref=partial.at[0], dst_ref=RB.at[k],
                send_sem=rs_send.at[0], recv_sem=rs_recv.at[k],
                device_id=device(k), device_id_type=MESH,
            )

        def gather(q, k):
            return pltpu.make_async_remote_copy(
                src_ref=GB.at[q], dst_ref=GB.at[q],
                send_sem=ag_send.at[k], recv_sem=ag_recv.at[q],
                device_id=device(k), device_id_type=MESH,
            )

        def others(stop, function):
            def one(k):
                @pl.when(k != flat)
                def _():
                    function(k)

            loop(0, stop, one)

        for q in range(owners):
            for h in range(2):
                cut = q * piece + h * half
                value = jnp.dot(
                    pooled, weight[:, cut:cut + half], preferred_element_type=F32
                ) + jnp.dot(
                    pooled, hot[:, :, cut:cut + half].reshape(Z * R, half),
                    preferred_element_type=F32,
                )
                partial[q, 4 * h:4 * h + 4] = value[0:4]

        def send(k):
            q = (flat + k) % count

            @pl.when(q < owners)
            def _():
                scatter(q).start()

        loop(1, count, send)

        @pl.when(flat < owners)
        def _():
            others(count, lambda k: scatter_from(k).wait_recv())
            RB[flat] = partial[flat]

            def add(k, total):
                return total + RB[k]

            GB[flat] = lax.fori_loop(1, count, add, RB[0])
            loop(1, count, lambda k: gather(flat, (flat + k) % count).start())

        others(owners, lambda q: gather(q, 0).wait_recv())
        for q in range(owners):
            read_ref[:, q * piece:q * piece + half] = GB[q, 0:3]
            read_ref[:, q * piece + half:(q + 1) * piece] = GB[q, 4:7]
        others(owners, lambda q: scatter(q).wait_send())

        @pl.when(flat < owners)
        def _():
            others(count, lambda k: gather(flat, k).wait_send())

    return kernel


def solution(mesh):
    sizes = tuple(mesh.shape[a] for a in AXES)
    count = sizes[0] * sizes[1] * sizes[2]

    def local(u_start, toughness, crack_label, obs_weight, sensor_cell):
        Z, R, C = toughness.shape
        S = sensor_cell.shape[0]
        owners = 1
        while owners * 2 <= count and S % (owners * 512) == 0:
            owners *= 2
        piece = S // owners
        n_dir = len(DIRECTIONS)
        any_spec = pl.BlockSpec(memory_space=pltpu.HBM)
        vmem_spec = pl.BlockSpec(memory_space=pltpu.VMEM)
        dma = pltpu.SemaphoreType.DMA
        return pl.pallas_call(
            make_kernel(Z, R, C, S, sizes, owners),
            out_shape=(
                jax.ShapeDtypeStruct((3, Z, R, C), F32),
                jax.ShapeDtypeStruct((Z, R, C), F32),
                jax.ShapeDtypeStruct((3, S), F32),
            ),
            in_specs=[any_spec] * 4 + [vmem_spec],
            out_specs=[vmem_spec] * 3,
            scratch_shapes=[
                pltpu.VMEM((2, 4, Z + 4, R + 8, C + 128), F32),
                pltpu.VMEM((2, 2, 4, Z + 2, R, 128), F32),
                pltpu.VMEM((2, 2, Z + 2, 8, C), F32),
                pltpu.VMEM((2, 2, Z, 8, C), F32),
                pltpu.VMEM((2, 2, 2, Z, 8, 128), F32),
                pltpu.VMEM((Z + 2, 3, R, C), F32),
                pltpu.VMEM((Z, R, C), F32),
                pltpu.VMEM((Z, R, C), jnp.int32),
                pltpu.VMEM((Z * R, S), jnp.bfloat16),
                pltpu.VMEM((Z * R, 128), F32),
                pltpu.VMEM((Z, R, S), jnp.bfloat16),
                pltpu.VMEM((owners, 8, piece // 2), F32),
                pltpu.VMEM((count, 8, piece // 2), F32),
                pltpu.VMEM((owners, 8, piece // 2), F32),
                dma((4,)),
                dma((2, n_dir, 2)),
                dma((2, n_dir, 2)),
                dma((owners,)),
                dma((count,)),
                dma((count,)),
                dma((owners,)),
            ],
            compiler_params=pltpu.CompilerParams(
                collective_id=0, has_side_effects=True, vmem_limit_bytes=40 * 1024 * 1024
            ),
            name="fracture",
        )(
            *[
                pltpu.with_memory_space_constraint(x, pltpu.HBM)
                for x in (u_start, toughness, crack_label, obs_weight.reshape(Z * R, S))
            ],
            sensor_cell.reshape(1, S),
        )

    return jax.shard_map(
        local,
        mesh=mesh,
        in_specs=(
            P(None, ("groups", "slab"), "pencil", "comp"),
            P(("groups", "slab"), "pencil", "comp"),
            P(("groups", "slab"), "pencil", "comp"),
            P("slab", "pencil", "comp", None),
            P(),
        ),
        out_specs=(
            P(None, ("groups", "slab"), "pencil", "comp"),
            P(("groups", "slab"), "pencil", "comp"),
            P(None, "groups"),
        ),
        check_vma=False,
    )
```

profile of v0, /device:TPU:0, one launch (start us, length us, event | category | flops | bytes accessed | tf_op | source)
XLA Modules:
  0.0 40.8 jit_solution(17969032033260575380)
XLA Ops:
  0.6 0.0 copy-start
  0.6 0.7 %copy-done = s32[4096]{0:T(1024)S(1)} copy-done((s32[4096]{0:T(1024)S(1)}, s32[4096]{0:T(1024)}, u32[]{:S(2)}) %copy-start) | copy-done | bytes 16408
  1.4 37.2 %fracture.1 = (f32[3,8,32,256]{3,2,1,0:T(8,128)S(1)}, f32[8,32,256]{2,1,0:T(8,128)S(1)}, f32[3,4096]{1,0:T(4,128)S(1)}) custom-call(f32[3,8,32,256]{3,2,1,0:T(8,128)} %u_hbm.1, f32[8,32,256]{2,1,0:T(8,128)} %tough_hbm.1, s32[8,32,256]{2,1,0:T(8,128)} %crack_hbm.1, bf16[256,4096]{1,0:T(8,128)(2,1)} %bitcast.3, s32[1,4096]{1,0:T(1,128)S(1)} %bitcast.2), custom_call_target="tpu_custom_call" | custom-call | tf_op jit(solution)/shard_map/fracture/pallas_call | solution.py:444
  38.6 0.9 %copy.11 = f32[3,8,32,256]{3,2,1,0:T(8,128)} copy(f32[3,8,32,256]{3,2,1,0:T(8,128)S(1)} %get-tuple-element.6) | data formatting | bytes 1572864
  39.5 0.7 %copy.12 = f32[8,32,256]{2,1,0:T(8,128)} copy(f32[8,32,256]{2,1,0:T(8,128)S(1)} %get-tuple-element.7) | data formatting | bytes 524288
  40.2 0.6 %copy.13 = f32[3,4096]{1,0:T(4,128)} copy(f32[3,4096]{1,0:T(4,128)S(1)} %get-tuple-element.8) | data formatting | bytes 98304
Async XLA Ops:
  0.6 0.7 %copy-start = (s32[4096]{0:T(1024)S(1)}, s32[4096]{0:T(1024)}, u32[]{:S(2)}) copy-start(s32[4096]{0:T(1024)} %param.9) | copy-start | bytes 49156
where the time goes:
time: 41 us; the launch traced here: 40.8 us
  Pallas kernels  37.2 us (91%)
  local copies, waits for them, and re-layouts  2.92 us (7%)
  between operations  0.65 us (2%)
    pallas_call x1, Pallas kernels, local(): pl.pallas_call(make_kernel(Z, R, C, S, sizes, owners), out_shape=(jax.Sha...  37.2 us
    unnamed x5, local copies, waits for them, and re-layouts  2.92 us

commit v1 on v0

v1 whole, which is shorter than its diff:
```python
import itertools

import jax
import jax.numpy as jnp
import numpy as np
from jax import lax
from jax.experimental import pallas as pl
from jax.experimental.pallas import tpu as pltpu
from jax.sharding import PartitionSpec as P

RESIDUAL_STIFF = 0.001
TIME_DISP = 0.15
TIME_DAMAGE = 0.08
DAMAGE_LEVEL = 0.45
POINT_GAIN = 8.0
AXES = ("slab", "pencil", "comp")
MESH = pl.DeviceIdType.MESH
F32 = jnp.float32


def third_angle_poly():
    nodes = 0.5 + 0.5 * np.cos(np.pi * (np.arange(200) + 0.5) / 200)
    fit = np.polynomial.chebyshev.Chebyshev.fit(
        nodes, np.cos(np.arccos(nodes) / 3.0), 8, domain=[0.0, 1.0]
    )
    return [float(c) for c in fit.convert(kind=np.polynomial.Polynomial).coef]


POLY = third_angle_poly()

DIRECTIONS = [
    d for d in itertools.product((-1, 0, 1), repeat=3) if 1 <= sum(map(abs, d)) <= 2
]
ALONG_Z = [d for d in DIRECTIONS if d[0] and not d[1] and not d[2]]
ALONG_Y = [d for d in DIRECTIONS if d[1] and not d[0] and not d[2]]
ALONG_X = [d for d in DIRECTIONS if d[2] and not d[0] and not d[1]]
DIAG_ZY = [d for d in DIRECTIONS if d[0] and d[1]]
DIAG_ZX = [d for d in DIRECTIONS if d[0] and d[2]]
DIAG_YX = [d for d in DIRECTIONS if d[1] and d[2]]
KINDS = (
    [("zu", d) for d in ALONG_Z] + [("zy", d) for d in DIAG_ZY] + [("zx", d) for d in DIAG_ZX]
    + [("zd", d) for d in ALONG_Z] + [("zs", d) for d in ALONG_Z]
    + [(k, d) for k in ("y0", "y1", "y2") for d in ALONG_Y]
    + [(k, d) for k in ("yx0", "yx1") for d in DIAG_YX]
    + [(k, d) for k in ("x0", "x1", "x2") for d in ALONG_X]
)
EDGE = ("zu", "zy", "zx")
REST = ("zd", "zs")


def energy_of(e00, e11, e22, e01, e02, e12):
    trace = e00 + e11 + e22
    mean = trace * (1.0 / 3.0)
    d0, d1, d2 = e00 - mean, e11 - mean, e22 - mean
    p2 = (d0 * d0 + d1 * d1 + d2 * d2) * (1.0 / 6.0) + (
        e01 * e01 + e02 * e02 + e12 * e12
    ) * (1.0 / 3.0)
    inv = lax.rsqrt(jnp.maximum(p2, 1e-36))
    p = p2 * inv
    b0, b1, b2 = d0 * inv, d1 * inv, d2 * inv
    b01, b02, b12 = e01 * inv, e02 * inv, e12 * inv
    half_det = 0.5 * (
        b0 * (b1 * b2 - b12 * b12)
        - b01 * (b01 * b2 - b12 * b02)
        + b02 * (b01 * b12 - b1 * b02)
    )
    r = jnp.minimum(jnp.abs(half_det), 1.0)
    c = jnp.full_like(r, POLY[-1])
    for coefficient in POLY[-2::-1]:
        c = c * r + coefficient
    tc = p * c
    t = jnp.where(half_det < 0.0, -tc, tc)
    s2 = jnp.maximum(1.0 - c * c, 0.0)
    delta = p * (s2 * lax.rsqrt(jnp.maximum(s2, 1e-30))) * float(np.sqrt(3.0))
    f1 = jnp.maximum(mean + 2.0 * t, 0.0)
    f2 = jnp.maximum(mean - t + delta, 0.0)
    f3 = jnp.maximum(mean - t - delta, 0.0)
    ft = jnp.maximum(trace, 0.0)
    return 0.75 * ft * ft + f1 * f1 + f2 * f2 + f3 * f3


def make_kernel(planes, rows, columns, sensors, sizes, first_owner, owners):
    n_slab, n_pencil, n_comp = sizes
    count = n_slab * n_pencil * n_comp
    Z, R, C = planes, rows, columns
    piece = sensors // owners
    half = piece // 2
    rim = 4 * R
    spans = {
        0: {"0": (0, Z)},
        1: {"0": (2, Z - 2), "1": (0, 2), "2": (Z - 2, Z)},
    }
    groups = {0: [range(Z)], 1: [range(2, Z - 2), [0, 1, Z - 2, Z - 1]]}
    near = n_slab <= 4 and n_pencil <= 2 and n_comp <= 2

    def scope(name):
        return jax.named_scope(name)

    def kernel(u_hbm, tough_hbm, crack_hbm, weight_hbm, cell_hbm,
               moved_ref, damage_ref, read_ref,
               U, XR, XS, XC, YR, YP, YZ, YX, YXR, TZ, tough, crack, weight, cell_ref, pooled_t, acc,
               partial, RB, GB,
               in_sem, send_sem, recv_sem, rs_send, rs_recv, ag_send, ag_recv):
        me = [lax.axis_index(a) for a in AXES]
        flat = (me[0] * n_pencil + me[1]) * n_comp + me[2]

        def device(index):
            return {
                "slab": index // (n_pencil * n_comp),
                "pencil": (index // n_comp) % n_pencil,
                "comp": index % n_comp,
            }

        def u_load(k, low, high):
            return pltpu.make_async_copy(
                u_hbm.at[:, low:high], U.at[0, 0:3, low + 2:high + 2, 0:R, 0:C], in_sem.at[k]
            )

        u_loads = [u_load(0, 0, 2), u_load(1, Z - 2, Z), u_load(2, 2, Z - 2)]
        crack_load = pltpu.make_async_copy(crack_hbm, crack, in_sem.at[3])
        tough_load = pltpu.make_async_copy(tough_hbm, tough, in_sem.at[4])
        cell_load = pltpu.make_async_copy(cell_hbm, cell_ref, in_sem.at[5])
        inner = Z * R - rim
        weight_loads = [
            pltpu.make_async_copy(weight_hbm.at[0:rim // 2], weight.at[0, 0:rim // 2], in_sem.at[6]),
            pltpu.make_async_copy(
                weight_hbm.at[Z * R - rim // 2:Z * R], weight.at[0, rim // 2:rim], in_sem.at[7]),
            pltpu.make_async_copy(
                weight_hbm.at[rim // 2:Z * R - rim // 2], weight.at[1, 0:inner], in_sem.at[8]),
        ]
        for load in [*u_loads, crack_load, cell_load, tough_load, *weight_loads]:
            load.start()

        barrier = pltpu.get_barrier_semaphore()

        def inside(d, sign):
            ok = None
            for m, o, n in zip(me, d, sizes):
                if o:
                    here = m + 1 < n if sign * o > 0 else m >= 1
                    ok = here if ok is None else jnp.logical_and(ok, here)
            return ok

        def feasible(d):
            return all(n > 1 for o, n in zip(d, sizes) if o)

        def neighbour(d):
            return {a: m + o for a, m, o in zip(AXES, me, d)}

        met = 0
        if near:
            for d in DIRECTIONS:
                if feasible(d):
                    @pl.when(inside(d, 1))
                    def _():
                        pl.semaphore_signal(
                            barrier, inc=1, device_id=neighbour(d), device_id_type=MESH
                        )

                    met = met + inside(d, 1).astype(jnp.int32)
        else:
            def greet(k, carry):
                pl.semaphore_signal(
                    barrier, inc=1, device_id=device((flat + k) % count), device_id_type=MESH
                )
                return carry

            lax.fori_loop(1, count, greet, 0)
            met = count - 1

        def clear(d, write):
            if feasible(d):
                @pl.when(jnp.logical_not(inside(d, 1)))
                def _():
                    write()
            else:
                write()

        def clear_z(up):
            def write():
                for step in range(2):
                    for z in ((Z + 2, Z + 3) if up else (0, 1)):
                        U[step, :, z, 0:R, 0:C] = jnp.zeros((4, R, C), F32)
                XC[:, up] = jnp.zeros((2, 2, R, 128), F32)
                for step in range(2):
                    for side in range(2):
                        YR[step, side, (Z + 1) * up] = jnp.zeros((8, C), F32)
            return write

        def clear_x(right):
            def write():
                def one(k, carry):
                    XR[k // (4 * Z), right, (k // Z) % 4, k % Z] = jnp.zeros((R, 128), F32)
                    return carry

                lax.fori_loop(0, 8 * Z, one, 0)
                XC[:, :, right] = jnp.zeros((2, 2, R, 128), F32)
                YXR[:, :, right] = jnp.zeros((2, 2, 2, 8, 128), F32)
            return write

        def clear_y(up):
            def write():
                YR[:, up] = jnp.zeros((2, Z + 2, 8, C), F32)
                YXR[:, up] = jnp.zeros((2, 2, 2, 8, 128), F32)
            return write

        for side, sign in ((0, -1), (1, 1)):
            clear((sign, 0, 0), clear_z(side))
            clear((0, sign, 0), clear_y(side))
            clear((0, 0, sign), clear_x(side))

        row8 = lax.broadcasted_iota(jnp.int32, (8, C), 0)
        row8t = lax.broadcasted_iota(jnp.int32, (8, 128), 0)
        lane8 = lax.broadcasted_iota(jnp.int32, (8, 128), 1)
        lane_r = lax.broadcasted_iota(jnp.int32, (R, 128), 1)

        def roll(value, shift, axis):
            shift = shift % value.shape[axis]
            return pltpu.roll(value, shift, axis) if shift else value

        def loop(start, stop, function):
            def one(z, carry):
                function(z)
                return carry

            lax.fori_loop(start, stop, one, 0)

        def message(step, kind, d):
            dz, dy, dx = d
            sz, sy, sx = (dz + 1) // 2, (dy + 1) // 2, (dx + 1) // 2
            lanes = slice(C - 128, C) if dx > 0 else slice(0, 128)
            edge = Z - 1 if dz > 0 else 0
            halo = 0 if dz > 0 else Z + 1
            if kind == "zu":
                pair = (U.at[step, 0:3, edge + 2, 0:R, 0:C], U.at[step, 0:3, halo + 1, 0:R, 0:C])
            elif kind == "zs":
                pair = (
                    U.at[step, 0:3, Z if dz > 0 else 3, 0:R, 0:C],
                    U.at[step, 0:3, 0 if dz > 0 else Z + 3, 0:R, 0:C],
                )
            elif kind == "zd":
                pair = (U.at[step, 3, edge + 2, 0:R, 0:C], U.at[step, 3, halo + 1, 0:R, 0:C])
            elif kind == "zy":
                pair = (YZ.at[step, sy, sz], YR.at[step, 1 - sy, halo])
            elif kind == "zx":
                pair = (XS.at[step, sz, sx], XC.at[step, 1 - sz, 1 - sx])
            elif kind[:2] == "yx":
                part = int(kind[2])
                pair = (YX.at[step, sy, sx, part], YXR.at[step, 1 - sy, 1 - sx, part])
            else:
                low, high = spans[step][kind[1]]
                if kind[0] == "y":
                    pair = (YP.at[step, sy, low:high], YR.at[step, 1 - sy, low + 1:high + 1])
                else:
                    pair = (
                        U.at[step, :, low + 2:high + 2, 0:R, lanes],
                        XR.at[step, 1 - sx, :, low:high],
                    )
            index = KINDS.index((kind, d))
            return pltpu.make_async_remote_copy(
                src_ref=pair[0],
                dst_ref=pair[1],
                send_sem=send_sem.at[step, index],
                recv_sem=recv_sem.at[step, index],
                device_id=neighbour(d),
                device_id_type=MESH,
            )

        def each(step, kinds, sign, action):
            for name in kinds:
                for kind, d in KINDS:
                    if kind == name and feasible(d):
                        @pl.when(inside(d, sign))
                        def _():
                            action(message(step, kind, d))

        def send(step, *kinds):
            each(step, kinds, 1, lambda copy: copy.start())

        def receive(step, *kinds):
            each(step, kinds, -1, lambda copy: copy.wait_recv())

        def pack_plane(step, z, save):
            low = [U[step, f, z + 2, 0:8, 0:C] for f in range(4)]
            high = [U[step, f, z + 2, R - 8:R, 0:C] for f in range(4)]
            for side, tiles, shifts in (
                (0, low, (0, 2, 4, 6)), (1, high, (2, 4, 6, 7))
            ):
                rolled = [roll(t, s, 0) for t, s in zip(tiles, shifts)]
                save(side, jnp.where(
                    row8 < 2, rolled[0],
                    jnp.where(row8 < 4, rolled[1], jnp.where(row8 < 6, rolled[2], rolled[3])),
                ))

        def pack_y(step, part):
            for z in groups[step][part]:
                def save(side, value):
                    YP[step, side, z] = value

                pack_plane(step, z, save)
            for side in range(2):
                for sx in range(2):
                    tile = jnp.zeros((8, 128), F32)
                    for z in groups[step][part]:
                        value = YP[step, side, z, :, (C - 128) * sx:(C - 128) * sx + 128]
                        tile = jnp.where(lane8 == z, roll(value, z + sx, 1), tile)
                    YX[step, side, sx, part] = tile

        def pack_corners(step):
            for sz, z in ((0, 0), (1, Z - 1)):
                for sx in range(2):
                    tiles = [
                        roll(U[step, f, z + 2, 0:R, (C - 128) * sx:(C - 128) * sx + 128], f + sx, 1)
                        for f in range(3)
                    ]
                    XS[step, sz, sx] = jnp.where(
                        lane_r == 0, tiles[0], jnp.where(lane_r == 1, tiles[1], tiles[2])
                    )

                def save(side, value):
                    YZ[step, side, sz] = value

                pack_plane(step, z, save)

        def merged(low, high, f, row):
            up, down = ((8 - 2 * f) % 8, 6 - 2 * f) if f < 3 else (2, 1)
            return jnp.where(row < 4, roll(high, up, 0), roll(low, down, 0))

        def unpack_x(step, z):
            for f in range(4):
                U[step, f, z + 2, 0:R, C:C + 128] = jnp.where(
                    lane_r < 64, XR[step, 1, f, z], XR[step, 0, f, z]
                )

        def unpack_zx(step):
            for sz, z in ((0, -1), (1, Z)):
                for f in range(3):
                    U[step, f, z + 2, 0:R, C:C + 128] = jnp.where(
                        lane_r < 64, roll(XC[step, sz, 1], -f, 1), roll(XC[step, sz, 0], 127 - f, 1)
                    )

        def unpack_y(step, z, fields):
            low, high = YR[step, 0, z + 1], YR[step, 1, z + 1]
            for f in range(fields):
                U[step, f, z + 2, R:R + 8, 0:C] = merged(low, high, f, row8)

        def unpack_yx(step, part):
            for z in groups[step][part]:
                left, right = [
                    [roll(YXR[step, sy, sx, part], 127 * (1 - sx) - z, 1) for sy in range(2)]
                    for sx in range(2)
                ]
                for f in range(3):
                    U[step, f, z + 2, R:R + 8, C:C + 128] = jnp.where(
                        lane8 < 64, merged(*right, f, row8t), merged(*left, f, row8t)
                    )

        def ends(step, z):
            now = [U[step, i, z + 2] for i in range(3)]
            gz = [
                U[step, i, z + 3, 0:R, 0:C] - U[step, i, z + 1, 0:R, 0:C] for i in range(3)
            ]

            def along(value, axis):
                return (roll(value, -1, axis) - roll(value, 1, axis))[0:R, 0:C]

            gy0, gy1 = along(now[0], 0), along(now[1], 0)
            gx0, gx2 = along(now[0], 1), along(now[2], 1)
            keep = 1.0 - U[step, 3, z + 2, 0:R, 0:C]
            g = (0.5 * TIME_DISP) * (keep * keep + RESIDUAL_STIFF)
            TZ[z + 1, 0] = g * (gz[0] + 0.75 * (gz[0] + gy1 + gx2))
            TZ[z + 1, 1] = g * (0.5 * (gz[1] + gy0))
            TZ[z + 1, 2] = g * (0.5 * (gz[2] + gx0))

        def store(step, f, z, value):
            if step == 0:
                U[1, f, z + 2, 0:R, 0:C] = value
            elif f < 3:
                moved_ref[f, z] = value
            else:
                damage_ref[z] = value

        def load(step, f, z):
            return U[1, f, z + 2, 0:R, 0:C] if step == 0 else moved_ref[f, z]

        def core(value):
            return value[0:R, 0:C]

        def hurt(step, z, gz0, gy1, gx2, s01, s02, s12):
            energy = energy_of(0.5 * gz0, 0.5 * gy1, 0.5 * gx2, 0.5 * s01, 0.5 * s02, 0.5 * s12)
            dy = U[step, 3, z + 2, :, 0:C]
            dx = U[step, 3, z + 2, 0:R]
            dc = U[step, 3, z + 2, 0:R, 0:C]
            lap = (
                U[step, 3, z + 3, 0:R, 0:C] + U[step, 3, z + 1, 0:R, 0:C]
                + (roll(dy, -1, 0) + roll(dy, 1, 0))[0:R]
                + (roll(dx, -1, 1) + roll(dx, 1, 1))[:, 0:C]
                - 6.0 * dc
            )
            store(step, 3, z, dc + TIME_DAMAGE * (
                2.0 * (1.0 - dc) * energy + tough[z] * (lap - dc)
            ))

        def damage(step, z):
            gz = [U[step, i, z + 3, 0:R, 0:C] - U[step, i, z + 1, 0:R, 0:C] for i in range(3)]
            in_rows = [U[step, i, z + 2, :, 0:C] for i in range(3)]
            in_lanes = [U[step, i, z + 2, 0:R, :] for i in range(3)]
            gy = [(roll(v, -1, 0) - roll(v, 1, 0))[0:R] for v in in_rows]
            gx = [(roll(v, -1, 1) - roll(v, 1, 1))[:, 0:C] for v in in_lanes]
            hurt(
                step, z, gz[0], gy[1], gx[2], 0.5 * (gz[1] + gy[0]), 0.5 * (gz[2] + gx[0]),
                0.5 * (gy[2] + gx[1]),
            )

        def force(step, z, with_damage):
            now = [U[step, i, z + 2] for i in range(3)]
            gz = [U[step, i, z + 3] - U[step, i, z + 1] for i in range(3)]
            gy = [roll(v, -1, 0) - roll(v, 1, 0) for v in now]
            gx = [roll(v, -1, 1) - roll(v, 1, 1) for v in now]
            keep = 1.0 - U[step, 3, z + 2]
            g = (0.5 * TIME_DISP) * (keep * keep + RESIDUAL_STIFF)
            lam = 0.75 * (gz[0] + gy[1] + gx[2])
            s01 = 0.5 * (gz[1] + gy[0])
            s02 = 0.5 * (gz[2] + gx[0])
            s12 = 0.5 * (gy[2] + gx[1])
            in_y = [g * s01, g * (gy[1] + lam), g * s12]
            in_x = [(g * s02)[0:R], in_y[2][0:R], (g * (gx[2] + lam))[0:R]]
            TZ[z + 1, 0] = core(g * (gz[0] + lam))
            TZ[z + 1, 1] = core(in_y[0])
            TZ[z + 1, 2] = in_x[0][:, 0:C]
            for i in range(3):
                ty = in_y[i][:, 0:C]
                change = (roll(ty, -1, 0) - roll(ty, 1, 0))[0:R] + (
                    roll(in_x[i], -1, 1) - roll(in_x[i], 1, 1)
                )[:, 0:C]
                store(step, i, z, core(now[i]) + change)
            if with_damage:
                hurt(step, z, core(gz[0]), core(gy[1]), core(gx[2]), core(s01), core(s02), core(s12))

        def finish(step, z):
            for i in range(3):
                store(step, i, z, load(step, i, z) + (TZ[z + 2, i] - TZ[z, i]))

        def finish_pool(z, row):
            means = []
            for i in range(3):
                value = moved_ref[i, z] + (TZ[z + 2, i] - TZ[z, i])
                moved_ref[i, z] = value
                folded = value[:, 0:128]
                for cut in range(128, C, 128):
                    folded = folded + value[:, cut:cut + 128]
                means.append(jnp.sum(folded, axis=1, keepdims=True) * (1.0 / C))
            pooled_t[row:row + R, :] = jnp.where(
                lane_r == 0, means[0], jnp.where(lane_r == 1, means[1], means[2])
            )

        def pooled(rows_here):
            value = pooled_t[0:rows_here, :].T[0:8].astype(jnp.bfloat16)
            return jnp.concatenate([value, value], axis=1)

        crack_load.wait()

        def label(z, carry):
            U[0, 3, z + 2, 0:R, 0:C] = DAMAGE_LEVEL * crack[z].astype(F32)
            return carry

        lax.fori_loop(0, Z, label, 0)
        u_loads[0].wait()
        u_loads[1].wait()
        pack_corners(0)
        with scope("barrier"):
            pl.semaphore_wait(barrier, met)
        send(0, "zu", "zx", "zy", "zd", "zs")
        u_loads[2].wait()
        with scope("pack"):
            pack_y(0, 0)
            send(0, "y0", "yx0", "x0")
        cell_load.wait()
        base = me[0] * Z * (R * n_pencil) + me[1] * R
        row_id = lax.broadcasted_iota(jnp.int32, (R, 512), 0) * n_comp

        def choose(part, z, row):
            start = (base + z * (R * n_pencil)) * n_comp + me[2]
            for s in range(0, sensors, 512):
                hit = row_id == cell_ref[:, s:s + 512] - start
                weight[part, row:row + R, s:s + 512] = jnp.where(hit, POINT_GAIN, 0.0).astype(
                    jnp.bfloat16
                )

        with scope("choose"):
            for k, z in enumerate((0, 1, Z - 2, Z - 1)):
                choose(0, z, rim + k * R)
            for z in range(2, Z - 2):
                choose(1, z, inner + (z - 2) * R)
            tough_load.wait()
        with scope("waitx"):
            receive(0, "x0")
        with scope("unpx"):
            loop(0, Z, lambda z: unpack_x(0, z))
        with scope("waity"):
            receive(0, "y0", "yx0")
        with scope("unpy"):
            loop(0, Z, lambda z: unpack_y(0, z, 4))
            unpack_yx(0, 0)
        with scope("body"):
            loop(1, Z - 1, lambda z: force(0, z, True))
            loop(2, Z - 2, lambda z: finish(0, z))
        with scope("pack1"):
            pack_y(1, 0)
            send(1, "y0", "yx0", "x0")
        with scope("waitza"):
            receive(0, *EDGE)
        with scope("edge"):
            unpack_zx(0)
            for z in (-1, Z):
                unpack_y(0, z, 3)
            loop(0, 2, lambda k: force(0, k * (Z - 1), False))
            loop(0, 2, lambda k: finish(0, 1 + k * (Z - 3)))
        send(1, "zs")
        with scope("waitzb"):
            receive(0, *REST)
        with scope("ends"):
            loop(0, 2, lambda k: ends(0, k * (Z + 1) - 1))
            loop(0, 2, lambda k: finish(0, k * (Z - 1)))
        pack_corners(1)
        send(1, "zu", "zx", "zy")
        with scope("damage"):
            loop(0, 2, lambda k: damage(0, k * (Z - 1)))
        send(1, "zd")
        with scope("pack2"):
            pack_y(1, 1)
            send(1, "y1", "y2", "yx1", "x1", "x2")

        with scope("waitx"):
            receive(1, "x0")
            loop(2, Z - 2, lambda z: unpack_x(1, z))
        with scope("waity"):
            receive(1, "y0", "yx0")
            loop(2, Z - 2, lambda z: unpack_y(1, z, 4))
            unpack_yx(1, 0)
        with scope("body"):
            loop(3, Z - 3, lambda z: force(1, z, False))
        with scope("waitxy"):
            receive(1, "x1", "x2", "y1", "y2", "yx1")
        with scope("unpxy"):
            for z in (0, 1, Z - 2, Z - 1):
                unpack_x(1, z)
                unpack_y(1, z, 4)
            unpack_yx(1, 1)
        with scope("body2"):
            loop(0, 2, lambda k: force(1, 1 + k * (Z - 3), False))
            loop(0, 2, lambda k: force(1, 2 + k * (Z - 5), False))
        with scope("pooli"):
            for z in range(2, Z - 2):
                finish_pool(z, (z - 2) * R)
        with scope("doti"):
            for load in weight_loads:
                load.wait()
            lhs = pooled(inner)
            for cut in range(0, sensors, 256):
                acc[:, cut:cut + 256] = jnp.dot(
                    lhs, weight[1, 0:2 * inner, cut:cut + 256], preferred_element_type=F32
                )
        with scope("waitz"):
            receive(1, *REST, *EDGE)
        with scope("edge"):
            unpack_zx(1)
            for z in (-1, Z):
                unpack_y(1, z, 3)
            loop(0, 2, lambda k: force(1, k * (Z - 1), False))
            loop(0, 2, lambda k: ends(1, k * (Z + 1) - 1))
        with scope("poole"):
            for k, z in enumerate((0, 1, Z - 2, Z - 1)):
                finish_pool(z, k * R)

        def spread(stop, function):
            if stop <= 16:
                for k in range(stop):
                    function(k)
            else:
                loop(0, stop, function)

        def scatter(q):
            return pltpu.make_async_remote_copy(
                src_ref=partial.at[q], dst_ref=RB.at[flat],
                send_sem=rs_send.at[q], recv_sem=rs_recv.at[flat],
                device_id=device(first_owner + q), device_id_type=MESH,
            )

        def scatter_from(k):
            return pltpu.make_async_remote_copy(
                src_ref=partial.at[0], dst_ref=RB.at[k],
                send_sem=rs_send.at[0], recv_sem=rs_recv.at[k],
                device_id=device(k), device_id_type=MESH,
            )

        def gather(q, k):
            return pltpu.make_async_remote_copy(
                src_ref=GB.at[q], dst_ref=GB.at[q],
                send_sem=ag_send.at[k], recv_sem=ag_recv.at[q],
                device_id=device(k), device_id_type=MESH,
            )

        def unless(same, function):
            @pl.when(jnp.logical_not(same))
            def _():
                function()

        mine = flat - first_owner
        owning = jnp.logical_and(mine >= 0, mine < owners)
        with scope("dot"):
            lhs = pooled(rim)
            for q in range(owners):
                for h in range(2):
                    cut = q * piece + h * half
                    value = acc[:, cut:cut + half] + jnp.dot(
                        lhs, weight[0, 0:2 * rim, cut:cut + half], preferred_element_type=F32
                    )
                    partial[q, 4 * h:4 * h + 4] = value[0:4]
                unless(mine == q, lambda: scatter(q).start())

        with scope("damage"):
            loop(0, Z, lambda z: damage(1, z))

        @pl.when(owning)
        def _():
            with scope("waitrs"):
                spread(count, lambda k: unless(flat == k, lambda: scatter_from(k).wait_recv()))
            RB[flat] = partial[mine]
            if count <= 16:
                total = RB[0]
                for k in range(1, count):
                    total = total + RB[k]
            else:
                total = lax.fori_loop(1, count, lambda k, t: t + RB[k], RB[0])
            GB[mine] = total
            spread(count, lambda k: unless(flat == k, lambda: gather(mine, k).start()))

        with scope("waitag"):
            for q in range(owners):
                unless(mine == q, lambda: gather(q, 0).wait_recv())
        for q in range(owners):
            read_ref[:, q * piece:q * piece + half] = GB[q, 0:3]
            read_ref[:, q * piece + half:(q + 1) * piece] = GB[q, 4:7]
        with scope("sends"):
            for step in range(2):
                names = ["zu", "zx", "zy", "zd", "zs", "y0", "yx0", "x0"]
                if step:
                    names += ["y1", "y2", "yx1", "x1", "x2"]
                each(step, names, 1, lambda copy: copy.wait_send())
            for q in range(owners):
                unless(mine == q, lambda: scatter(q).wait_send())

            @pl.when(owning)
            def _():
                spread(count, lambda k: unless(flat == k, lambda: gather(mine, k).wait_send()))

    return kernel


def emit(moved_ref, damage_ref, read_ref, moved_hbm, damage_hbm, read_hbm, sem):
    copies = [
        pltpu.make_async_copy(moved_ref, moved_hbm, sem.at[0]),
        pltpu.make_async_copy(damage_ref, damage_hbm, sem.at[1]),
        pltpu.make_async_copy(read_ref, read_hbm, sem.at[2]),
    ]
    for copy in copies:
        copy.start()
    for copy in copies:
        copy.wait()


def solution(mesh):
    sizes = tuple(mesh.shape[a] for a in AXES)
    n_slab, plane_devices = sizes[0], sizes[1] * sizes[2]
    count = n_slab * plane_devices

    def local(u_start, toughness, crack_label, obs_weight, sensor_cell):
        Z, R, C = toughness.shape
        S = sensor_cell.shape[0]
        first_owner = max(n_slab // 2 - 1, 0) * plane_devices
        owners = min(2, n_slab) * plane_devices
        while S % (owners * 256):
            owners -= 1
        piece = S // owners
        rim, inner = 4 * R, (Z - 4) * R
        any_spec = pl.BlockSpec(memory_space=pltpu.HBM)
        vmem_spec = pl.BlockSpec(memory_space=pltpu.VMEM)
        dma = pltpu.SemaphoreType.DMA
        shapes = (
            jax.ShapeDtypeStruct((3, Z, R, C), F32),
            jax.ShapeDtypeStruct((Z, R, C), F32),
            jax.ShapeDtypeStruct((3, S), F32),
        )
        outs = pl.pallas_call(
            make_kernel(Z, R, C, S, sizes, first_owner, owners),
            out_shape=shapes,
            in_specs=[any_spec] * 5,
            out_specs=[vmem_spec] * 3,
            scratch_shapes=[
                pltpu.VMEM((2, 4, Z + 4, R + 8, C + 128), F32),
                pltpu.VMEM((2, 2, 4, Z, R, 128), F32),
                pltpu.VMEM((2, 2, 2, R, 128), F32),
                pltpu.VMEM((2, 2, 2, R, 128), F32),
                pltpu.VMEM((2, 2, Z + 2, 8, C), F32),
                pltpu.VMEM((2, 2, Z, 8, C), F32),
                pltpu.VMEM((2, 2, 2, 8, C), F32),
                pltpu.VMEM((2, 2, 2, 2, 8, 128), F32),
                pltpu.VMEM((2, 2, 2, 2, 8, 128), F32),
                pltpu.VMEM((Z + 2, 3, R, C), F32),
                pltpu.VMEM((Z, R, C), F32),
                pltpu.VMEM((Z, R, C), jnp.int32),
                pltpu.VMEM((2, 2 * max(rim, inner), S), jnp.bfloat16),
                pltpu.VMEM((1, S), jnp.int32),
                pltpu.VMEM((max(rim, inner), 128), F32),
                pltpu.VMEM((8, S), F32),
                pltpu.VMEM((owners, 8, piece // 2), F32),
                pltpu.VMEM((count, 8, piece // 2), F32),
                pltpu.VMEM((owners, 8, piece // 2), F32),
                dma((9,)),
                dma((2, len(KINDS))),
                dma((2, len(KINDS))),
                dma((owners,)),
                dma((count,)),
                dma((count,)),
                dma((owners,)),
            ],
            compiler_params=pltpu.CompilerParams(
                collective_id=0, has_side_effects=True, vmem_limit_bytes=40 * 1024 * 1024
            ),
            name="fracture",
        )(
            *[
                pltpu.with_memory_space_constraint(x, pltpu.HBM)
                for x in (
                    u_start, toughness, crack_label, obs_weight.reshape(Z * R, S),
                    sensor_cell.reshape(1, S),
                )
            ],
        )
        return pl.pallas_call(
            emit,
            out_shape=shapes,
            in_specs=[vmem_spec] * 3,
            out_specs=[any_spec] * 3,
            scratch_shapes=[dma((3,))],
            name="emit",
        )(*[pltpu.with_memory_space_constraint(x, pltpu.VMEM) for x in outs])

    return jax.shard_map(
        local,
        mesh=mesh,
        in_specs=(
            P(None, ("groups", "slab"), "pencil", "comp"),
            P(("groups", "slab"), "pencil", "comp"),
            P(("groups", "slab"), "pencil", "comp"),
            P("slab", "pencil", "comp", None),
            P(),
        ),
        out_specs=(
            P(None, ("groups", "slab"), "pencil", "comp"),
            P(("groups", "slab"), "pencil", "comp"),
            P(None, "groups"),
        ),
        check_vma=False,
    )
```

time: 41 us -> 32.1 us (0.78)
  Pallas kernels: 37.2 us -> 31.3 us
  local copies, waits for them, and re-layouts: 2.92 us -> 0 us
    pallas_call x1 -> x2, Pallas kernels: 37.2 us -> 31.3 us  [the longest x1 30.3 us: local(): pl.pallas_call(make_kernel(Z, R, C, S, sizes, first_owner, owners), out_s...]
    unnamed x5 -> x0, local copies, waits for them, and re-layouts: 2.92 us -> none
where the time goes in v1:
time: 32.1 us; the launch traced here: 31.9 us
  Pallas kernels  31.3 us (98%)
  between operations  0.64 us (2%)
    pallas_call x1, Pallas kernels, local(): pl.pallas_call(make_kernel(Z, R, C, S, sizes, first_owner, owners), out_s...  30.3 us
    pallas_call x1, Pallas kernels, local(): pl.pallas_call(emit, out_shape=shapes, in_specs=[vmem_spec] * 3, out_spec...  1 us

profile of v1, /device:TPU:0, one launch (start us, length us, event | category | flops | bytes accessed | tf_op | source)
XLA Modules:
  0.0 31.9 jit_solution(12952328416222519917)
XLA Ops:
  0.6 30.3 %fracture.1 = (f32[3,8,32,256]{3,2,1,0:T(8,128)S(1)}, f32[8,32,256]{2,1,0:T(8,128)S(1)}, f32[3,4096]{1,0:T(4,128)S(1)}) custom-call(f32[3,8,32,256]{3,2,1,0:T(8,128)} %u_hbm.1, f32[8,32,256]{2,1,0:T(8,128)} %tough_hbm.1, s32[8,32,256]{2,1,0:T(8,128)} %crack_hbm.1, bf16[256,4096]{1,0:T(8,128)(2,1)} %bitcast.2, s32[1,4096]{1,0:T(1,128)} %bitcast.3), custom_call_target="tpu_custom_call" | custom-call | tf_op jit(solution)/shard_map/fracture/pallas_call | solution.py:695
  30.9 1.0 %emit.1 = (f32[3,8,32,256]{3,2,1,0:T(8,128)}, f32[8,32,256]{2,1,0:T(8,128)}, f32[3,4096]{1,0:T(4,128)}) custom-call(f32[3,8,32,256]{3,2,1,0:T(8,128)S(1)} %get-tuple-element.6.moved_ref, f32[8,32,256]{2,1,0:T(8,128)S(1)} %get-tuple-element.7.damage_ref, f32[3,4096]{1,0:T(4,128)S(1)} %get-tuple-element.8.read_ref), custom_call_target="tpu_custom_call" | custom-call | tf_op jit(solution)/shard_map/emit/pallas_call | solution.py:741

commit v2 on v1

v2 whole, which is shorter than its diff:
```python
import itertools

import jax
import jax.numpy as jnp
import numpy as np
from jax import lax
from jax.experimental import pallas as pl
from jax.experimental.pallas import tpu as pltpu
from jax.sharding import PartitionSpec as P

RESIDUAL_STIFF = 0.001
TIME_DISP = 0.15
TIME_DAMAGE = 0.08
DAMAGE_LEVEL = 0.45
POINT_GAIN = 8.0
AXES = ("slab", "pencil", "comp")
MESH = pl.DeviceIdType.MESH
F32 = jnp.float32


def third_angle_poly():
    nodes = 0.5 + 0.5 * np.cos(np.pi * (np.arange(200) + 0.5) / 200)
    fit = np.polynomial.chebyshev.Chebyshev.fit(
        nodes, np.cos(np.arccos(nodes) / 3.0), 8, domain=[0.0, 1.0]
    )
    return [float(c) for c in fit.convert(kind=np.polynomial.Polynomial).coef]


POLY = third_angle_poly()

DIRECTIONS = [
    d for d in itertools.product((-1, 0, 1), repeat=3) if 1 <= sum(map(abs, d)) <= 2
]
ALONG_Z = [d for d in DIRECTIONS if d[0] and not d[1] and not d[2]]
ALONG_Y = [d for d in DIRECTIONS if d[1] and not d[0] and not d[2]]
ALONG_X = [d for d in DIRECTIONS if d[2] and not d[0] and not d[1]]
DIAG_ZY = [d for d in DIRECTIONS if d[0] and d[1]]
DIAG_ZX = [d for d in DIRECTIONS if d[0] and d[2]]
DIAG_YX = [d for d in DIRECTIONS if d[1] and d[2]]
KINDS = (
    [("zu", d) for d in ALONG_Z] + [("zy", d) for d in DIAG_ZY] + [("zx", d) for d in DIAG_ZX]
    + [("zd", d) for d in ALONG_Z] + [("zs", d) for d in ALONG_Z]
    + [(k, d) for k in ("y0", "y1", "y2") for d in ALONG_Y]
    + [(k, d) for k in ("yx0", "yx1") for d in DIAG_YX]
    + [(k, d) for k in ("x0", "x1", "x2") for d in ALONG_X]
)
EDGE = ("zu", "zy", "zx")
REST = ("zd", "zs")


def energy_of(g0, g1, g2, a01, a02, a12):
    trace = g0 + g1 + g2
    mean = trace * (1.0 / 3.0)
    d0, d1, d2 = g0 - mean, g1 - mean, g2 - mean
    q01, q02, q12 = a01 * a01, a02 * a02, a12 * a12
    d01 = d0 * d1
    p2 = (d0 * d0 + d1 * d1 + d01) * (1.0 / 3.0) + (q01 + q02 + q12) * (1.0 / 12.0)
    inv = lax.rsqrt(jnp.maximum(p2, 1e-36))
    p = p2 * inv
    det = d01 * d2 + 0.25 * (a01 * a02 * a12 - d0 * q12 - d1 * q02 - d2 * q01)
    half_det = ((det * inv) * inv) * (0.5 * inv)
    r = jnp.minimum(jnp.abs(half_det), 1.0)
    c = jnp.full_like(r, POLY[-1])
    for coefficient in POLY[-2::-1]:
        c = c * r + coefficient
    tc = p * c
    t = jnp.where(half_det < 0.0, -tc, tc)
    s2 = jnp.maximum(1.0 - c * c, 0.0)
    delta = p * (s2 * lax.rsqrt(jnp.maximum(s2, 1e-30))) * float(np.sqrt(3.0))
    f1 = jnp.maximum(mean + 2.0 * t, 0.0)
    f2 = jnp.maximum(mean - t + delta, 0.0)
    f3 = jnp.maximum(mean - t - delta, 0.0)
    ft = jnp.maximum(trace, 0.0)
    return 0.75 * ft * ft + f1 * f1 + f2 * f2 + f3 * f3


def message_tiles(kind, step, Z, R, L):
    if kind in ("zu", "zs"):
        return 3 * L * R // 8
    if kind == "zd":
        return L * R // 8
    if kind == "zx":
        return R // 8
    if kind == "zy":
        return L
    if kind[:2] == "yx":
        return 1
    planes = 2 if kind[1] != "0" else Z - 4 if step else Z
    return planes * L if kind[0] == "y" else planes * 4 * R // 8


SENT = [
    ("zu", "zx", "zy", "zd", "zs", "y0", "yx0", "x0"),
    ("zu", "zx", "zy", "zd", "zs", "y0", "yx0", "x0", "y1", "y2", "yx1", "x1", "x2"),
]


def group_tiles(step, kinds, met, Z, R, L):
    total = 0
    for kind in kinds:
        number = message_tiles(kind, step, Z, R, L)
        axes = [a for a, name in enumerate("zyx") if name in kind[:2]]
        for a in axes if kind[:2] in ("zx", "zy", "yx") else axes[:1]:
            number *= met[a]
        total += number
    return total


def make_kernel(planes, rows, columns, sensors, sizes, first_slab, owners):
    n_slab, n_pencil, n_comp = sizes
    count = n_slab * n_pencil * n_comp
    Z, R, C = planes, rows, columns
    piece = sensors // owners
    strips = piece // 128
    L = C // 128
    TOP = 16
    END = TOP + R
    body_rows = slice(TOP, END)
    rim = 4 * R
    spans = {
        0: {"0": (0, Z)},
        1: {"0": (2, Z - 2), "1": (0, 2), "2": (Z - 2, Z)},
    }
    groups = {0: [range(Z)], 1: [range(2, Z - 2), [0, 1, Z - 2, Z - 1]]}
    near = n_slab <= 4 and n_pencil <= 2 and n_comp <= 2

    def scope(name):
        return jax.named_scope(name)

    def kernel(u_hbm, tough_hbm, crack_hbm, weight_hbm, cell_hbm,
               moved_ref, damage_ref, read_ref,
               U, XR, XS, XC, YR, YP, YZ, YX, YXR, TZ, TY, W, tough, crack, weight, cell_ref, pooled_t, acc,
               partial, RB, GB,
               in_sem, send_sem, recv_sem):
        me = [lax.axis_index(a) for a in AXES]
        flat = (me[0] * n_pencil + me[1]) * n_comp + me[2]

        def device(index):
            return {
                "slab": index // (n_pencil * n_comp),
                "pencil": (index // n_comp) % n_pencil,
                "comp": index % n_comp,
            }

        def u_load(k, low, high):
            return [
                pltpu.make_async_copy(
                    u_hbm.at[:, low:high, :, 128 * l:128 * l + 128],
                    U.at[0, 0:3, low + 2:high + 2, l, body_rows, :],
                    in_sem.at[4 if k == 2 else 0],
                )
                for l in range(L)
            ]

        edge_loads = u_load(0, 0, 2) + u_load(1, Z - 2, Z)
        inner_loads = u_load(2, 2, Z - 2)
        crack_load = pltpu.make_async_copy(crack_hbm, crack, in_sem.at[1])
        tough_load = pltpu.make_async_copy(tough_hbm, tough, in_sem.at[2])
        cell_load = pltpu.make_async_copy(cell_hbm, cell_ref, in_sem.at[3])
        inner = Z * R - rim
        weight_loads = [
            pltpu.make_async_copy(weight_hbm.at[0:rim // 2], weight.at[0, 0:rim // 2], in_sem.at[5]),
            pltpu.make_async_copy(
                weight_hbm.at[Z * R - rim // 2:Z * R], weight.at[0, rim // 2:rim], in_sem.at[5]),
            pltpu.make_async_copy(
                weight_hbm.at[rim // 2:Z * R - rim // 2], weight.at[1, 0:inner], in_sem.at[5]),
        ]
        for item in [*edge_loads, crack_load, *inner_loads, cell_load]:
            item.start()

        barrier = pltpu.get_barrier_semaphore()

        def inside(d, sign):
            ok = None
            for m, o, n in zip(me, d, sizes):
                if o:
                    here = m + 1 < n if sign * o > 0 else m >= 1
                    ok = here if ok is None else jnp.logical_and(ok, here)
            return ok

        def feasible(d):
            return all(n > 1 for o, n in zip(d, sizes) if o)

        def neighbour(d):
            return {a: m + o for a, m, o in zip(AXES, me, d)}

        met = 0
        if near:
            for d in DIRECTIONS:
                if feasible(d):
                    @pl.when(inside(d, 1))
                    def _():
                        pl.semaphore_signal(
                            barrier, inc=1, device_id=neighbour(d), device_id_type=MESH
                        )

                    met = met + inside(d, 1).astype(jnp.int32)
        else:
            def greet(k, carry):
                pl.semaphore_signal(
                    barrier, inc=1, device_id=device((flat + k) % count), device_id_type=MESH
                )
                return carry

            lax.fori_loop(1, count, greet, 0)
            met = count - 1

        def clear(d, write):
            if feasible(d):
                @pl.when(jnp.logical_not(inside(d, 1)))
                def _():
                    write()
            else:
                write()

        def clear_z(up):
            def write():
                for step in range(2):
                    for z in ((Z + 2, Z + 3) if up else (0, 1)):
                        U[step, :, z, 0:L, body_rows] = jnp.zeros((4, L, R, 128), F32)
                XC[:, up] = jnp.zeros((2, 2, R, 128), F32)
                for step in range(2):
                    for side in range(2):
                        YR[step, side, (Z + 1) * up] = jnp.zeros((8, C), F32)
            return write

        def clear_x(right):
            def write():
                def one(k, carry):
                    XR[k // (4 * Z), right, (k // Z) % 4, k % Z] = jnp.zeros((R, 128), F32)
                    return carry

                lax.fori_loop(0, 8 * Z, one, 0)
                XC[:, :, right] = jnp.zeros((2, 2, R, 128), F32)
                YXR[:, :, right] = jnp.zeros((2, 2, 2, 8, 128), F32)
            return write

        def clear_y(up):
            def write():
                YR[:, up] = jnp.zeros((2, Z + 2, 8, C), F32)
                YXR[:, up] = jnp.zeros((2, 2, 2, 8, 128), F32)
            return write

        row8t = lax.broadcasted_iota(jnp.int32, (8, 128), 0)
        lane8 = lax.broadcasted_iota(jnp.int32, (8, 128), 1)
        lane_r = lax.broadcasted_iota(jnp.int32, (R, 128), 1)

        def roll(value, shift, axis):
            shift = shift % value.shape[axis]
            return pltpu.roll(value, shift, axis) if shift else value

        def loop(start, stop, function):
            def one(z, carry):
                function(z)
                return carry

            lax.fori_loop(start, stop, one, 0)

        def slot(step, kind):
            if step == 0:
                return 0 if kind in EDGE else 1 if kind in REST else 2 if kind[0] == "x" else 3
            if kind[0] == "z":
                return 4
            return 7 if kind[-1] != "0" else 5 if kind[0] == "x" else 6

        def message(step, kind, d):
            dz, dy, dx = d
            sz, sy, sx = (dz + 1) // 2, (dy + 1) // 2, (dx + 1) // 2
            tile = L - 1 if dx > 0 else 0
            edge = Z - 1 if dz > 0 else 0
            halo = 0 if dz > 0 else Z + 1
            if kind == "zu":
                pair = (
                    U.at[step, 0:3, edge + 2, 0:L, body_rows], U.at[step, 0:3, halo + 1, 0:L, body_rows]
                )
            elif kind == "zs":
                pair = (
                    U.at[step, 0:3, Z if dz > 0 else 3, 0:L, body_rows],
                    U.at[step, 0:3, 0 if dz > 0 else Z + 3, 0:L, body_rows],
                )
            elif kind == "zd":
                pair = (U.at[step, 3, edge + 2, 0:L, body_rows], U.at[step, 3, halo + 1, 0:L, body_rows])
            elif kind == "zy":
                pair = (YZ.at[step, sy, sz], YR.at[step, 1 - sy, halo])
            elif kind == "zx":
                pair = (XS.at[step, sz, sx], XC.at[step, 1 - sz, 1 - sx])
            elif kind[:2] == "yx":
                part = int(kind[2])
                pair = (YX.at[step, sy, sx, part], YXR.at[step, 1 - sy, 1 - sx, part])
            else:
                low, high = spans[step][kind[1]]
                if kind[0] == "y":
                    pair = (YP.at[step, sy, low:high], YR.at[step, 1 - sy, low + 1:high + 1])
                else:
                    pair = (
                        U.at[step, :, low + 2:high + 2, tile, body_rows],
                        XR.at[step, 1 - sx, :, low:high],
                    )
            return pltpu.make_async_remote_copy(
                src_ref=pair[0],
                dst_ref=pair[1],
                send_sem=send_sem.at[0],
                recv_sem=recv_sem.at[slot(step, kind)],
                device_id=neighbour(d),
                device_id_type=MESH,
            )

        def each(step, kinds, sign, action):
            for name in kinds:
                for kind, d in KINDS:
                    if kind == name and feasible(d):
                        @pl.when(inside(d, sign))
                        def _():
                            action(message(step, kind, d))

        def settle(tiles, sem):
            if tiles:
                pltpu.make_async_copy(W.at[0:tiles], W.at[0:tiles], sem).wait()

        def settle_messages(steps, kinds, sem):
            for number in itertools.product(*[
                (0,) if n == 1 else (1,) if n == 2 else (1, 2) for n in sizes
            ]):
                here = None
                for m, n, k in zip(me, sizes, number):
                    if n > 2:
                        both = jnp.logical_and(m > 0, m < n - 1)
                        ok = both if k == 2 else jnp.logical_not(both)
                        here = ok if here is None else jnp.logical_and(here, ok)
                tiles = sum(group_tiles(t, kinds(t), number, Z, R, L) for t in steps)

                def wait():
                    settle(tiles, sem)

                if here is None:
                    wait()
                else:
                    pl.when(here)(wait)

        def send(step, *kinds):
            each(step, kinds, 1, lambda copy: copy.start())

        def receive(step, *kinds):
            settle_messages((step,), lambda _: kinds, recv_sem.at[slot(step, kinds[0])])

        def pack_plane(step, z, save):
            for side, firsts in (
                (0, [TOP - 2 * f for f in range(4)]),
                (1, [END - 2 - 2 * f for f in range(3)] + [END - 7]),
            ):
                for l in range(L):
                    rows = [U[step, f, z + 2, l, at:at + 8, :] for f, at in enumerate(firsts)]
                    save(side, l, jnp.where(
                        row8t < 2, rows[0],
                        jnp.where(row8t < 4, rows[1], jnp.where(row8t < 6, rows[2], rows[3])),
                    ))

        def pack_y(step, part):
            for z in groups[step][part]:
                def save(side, l, value):
                    YP[step, side, z, :, 128 * l:128 * l + 128] = value

                pack_plane(step, z, save)
            for side in range(2):
                for sx in range(2):
                    tile = jnp.zeros((8, 128), F32)
                    for z in groups[step][part]:
                        value = YP[step, side, z, :, (C - 128) * sx:(C - 128) * sx + 128]
                        tile = jnp.where(lane8 == z, roll(value, z + sx, 1), tile)
                    YX[step, side, sx, part] = tile

        def pack_corners(step):
            for sz, z in ((0, 0), (1, Z - 1)):
                for sx in range(2):
                    tiles = [
                        roll(U[step, f, z + 2, (L - 1) * sx, body_rows, :], f + sx, 1)
                        for f in range(3)
                    ]
                    XS[step, sz, sx] = jnp.where(
                        lane_r == 0, tiles[0], jnp.where(lane_r == 1, tiles[1], tiles[2])
                    )

                def save(side, l, value):
                    YZ[step, side, sz, :, 128 * l:128 * l + 128] = value

                pack_plane(step, z, save)

        def unpack_x(step, z):
            for f in range(4):
                U[step, f, z + 2, L, body_rows, :] = jnp.where(
                    lane_r < 64, XR[step, 1, f, z], XR[step, 0, f, z]
                )

        def unpack_zx(step):
            for sz, z in ((0, -1), (1, Z)):
                for f in range(3):
                    U[step, f, z + 2, L, body_rows, :] = jnp.where(
                        lane_r < 64, roll(XC[step, sz, 1], -f, 1), roll(XC[step, sz, 0], 127 - f, 1)
                    )

        def put_rows(step, z, l, low, high, fields):
            for f in range(fields):
                if f < 3:
                    U[step, f, z + 2, l, TOP - 2:TOP, :] = low[2 * f:2 * f + 2]
                    U[step, f, z + 2, l, END:END + 2, :] = high[2 * f:2 * f + 2]
                else:
                    U[step, f, z + 2, l, TOP - 1:TOP, :] = low[6:7]
                    U[step, f, z + 2, l, END:END + 1, :] = high[6:7]

        def unpack_y(step, z, fields):
            for l in range(L):
                low, high = [YR[step, side, z + 1, :, 128 * l:128 * l + 128] for side in range(2)]
                put_rows(step, z, l, low, high, fields)

        def unpack_yx(step, part):
            for z in groups[step][part]:
                low, high = [
                    jnp.where(
                        lane8 < 64, roll(YXR[step, sy, 1, part], -z, 1),
                        roll(YXR[step, sy, 0, part], 127 - z, 1),
                    )
                    for sy in range(2)
                ]
                put_rows(step, z, L, low, high, 3)

        def take(step, f, z, row, tiles):
            parts = [U[step, f, z, l, row:row + 8, :] for l in range(tiles)]
            return jnp.concatenate(parts, axis=1)

        def slope_z(step, f, z, row, tiles):
            return take(step, f, z + 3, row, tiles) - take(step, f, z + 1, row, tiles)

        def slope_y(step, f, z, row, tiles):
            return take(step, f, z + 2, row + 1, tiles) - take(step, f, z + 2, row - 1, tiles)

        def beside(value, tiles):
            parts = [value[:, 128 * l:128 * l + 128] for l in range(L + 1)]
            after, before = [], []
            for l in range(tiles):
                after.append(roll(jnp.where(lane8 == 0, parts[(l + 1) % (L + 1)], parts[l]), -1, 1))
                before.append(roll(jnp.where(lane8 == 127, parts[l - 1], parts[l]), 1, 1))
            return jnp.concatenate(after, axis=1), jnp.concatenate(before, axis=1)

        def along_x(value, tiles):
            after, before = beside(value, tiles)
            return after - before

        def slope_x(step, f, z, row):
            return along_x(take(step, f, z + 2, row, L + 1), L)

        def gain(step, z, row, tiles):
            keep = 1.0 - take(step, 3, z + 2, row, tiles)
            return (0.5 * TIME_DISP) * (keep * keep + RESIDUAL_STIFF)

        def store(step, f, z, row, value):
            if step == 0:
                for l in range(L):
                    U[1, f, z + 2, l, row:row + 8, :] = value[:, 128 * l:128 * l + 128]
            elif f < 3:
                moved_ref[f, z, row - TOP:row - TOP + 8, :] = value
            else:
                damage_ref[z, row - TOP:row - TOP + 8, :] = value

        core_rows = range(TOP, END, 8)

        def ends(step, z):
            for row in core_rows:
                gz = [slope_z(step, f, z, row, L) for f in range(3)]
                gy0, gy1 = slope_y(step, 0, z, row, L), slope_y(step, 1, z, row, L)
                gx0, gx2 = slope_x(step, 0, z, row), slope_x(step, 2, z, row)
                g = gain(step, z, row, L)
                h = 0.5 * g
                at = slice(row - TOP, row - TOP + 8)
                TZ[z + 1, 0, at] = g * (gz[0] + 0.75 * (gz[0] + gy1 + gx2))
                TZ[z + 1, 1, at] = h * (gz[1] + gy0)
                TZ[z + 1, 2, at] = h * (gz[2] + gx0)

        def hurt(step, z, row, gz0, gy1, gx2, a01, a02, a12):
            energy = energy_of(gz0, gy1, gx2, a01, a02, a12)
            dx = take(step, 3, z + 2, row, L + 1)
            dc = dx[:, 0:C]
            after, before = beside(dx, L)
            lap = (
                take(step, 3, z + 3, row, L) + take(step, 3, z + 1, row, L)
                + take(step, 3, z + 2, row + 1, L) + take(step, 3, z + 2, row - 1, L)
                + (after + before)
                - 7.0 * dc
            )
            store(step, 3, z, row, dc + TIME_DAMAGE * (
                0.5 * (1.0 - dc) * energy + tough[z, row - TOP:row - TOP + 8, :] * lap
            ))

        def damage(step, z):
            for row in core_rows:
                gz = [slope_z(step, f, z, row, L) for f in range(3)]
                gy = [slope_y(step, f, z, row, L) for f in range(3)]
                gx = [slope_x(step, f, z, row) for f in range(3)]
                hurt(
                    step, z, row, gz[0], gy[1], gx[2],
                    gz[1] + gy[0], gz[2] + gx[0], gy[2] + gx[1],
                )

        def put_y(row, values):
            for i in range(3):
                for l in range(L):
                    TY[i, l, row:row + 8, :] = values[i][:, 128 * l:128 * l + 128]

        def force(step, z, with_damage):
            for row in (TOP - 8, END):
                gy = [slope_y(step, f, z, row, L) for f in range(3)]
                gx1, gx2 = [slope_x(step, f, z, row) for f in (1, 2)]
                gz0, gz1 = [slope_z(step, f, z, row, L) for f in (0, 1)]
                g = gain(step, z, row, L)
                h = 0.5 * g
                put_y(row, [
                    h * (gz1 + gy[0]), g * (gy[1] + 0.75 * (gz0 + gy[1] + gx2)), h * (gy[2] + gx1)
                ])

            def close(row, waiting):
                for i in range(3):
                    change = jnp.concatenate(
                        [TY[i, l, row + 1:row + 9, :] - TY[i, l, row - 1:row + 7, :] for l in range(L)],
                        axis=1,
                    )
                    store(step, i, z, row, waiting[i] + change)

            waiting = None
            for row in core_rows:
                wide = L + 1
                now = [take(step, f, z + 2, row, wide) for f in range(3)]
                gz = [slope_z(step, f, z, row, wide) for f in range(3)]
                gy = [slope_y(step, f, z, row, wide) for f in range(3)]
                gx = [along_x(v, wide) for v in now]
                g = gain(step, z, row, wide)
                h = 0.5 * g
                lam = 0.75 * (gz[0] + gy[1] + gx[2])
                a01 = (gz[1] + gy[0])[:, 0:C]
                a02 = gz[2] + gx[0]
                a12 = gy[2] + gx[1]
                t01, t02, t12 = h[:, 0:C] * a01, h * a02, h * a12
                put_y(row, [t01, (g * (gy[1] + lam))[:, 0:C], t12[:, 0:C]])
                at = slice(row - TOP, row - TOP + 8)
                TZ[z + 1, 0, at] = (g * (gz[0] + lam))[:, 0:C]
                TZ[z + 1, 1, at] = t01
                TZ[z + 1, 2, at] = t02[:, 0:C]
                ready = [
                    now[i][:, 0:C] + along_x(t, L)
                    for i, t in enumerate((t02, t12, g * (gx[2] + lam)))
                ]
                if waiting is not None:
                    close(row - 8, waiting)
                waiting = ready
                if with_damage:
                    hurt(
                        step, z, row, gz[0][:, 0:C], gy[1][:, 0:C], gx[2][:, 0:C],
                        a01, a02[:, 0:C], a12[:, 0:C],
                    )
            close(END - 8, waiting)

        def finish(step, z):
            for i in range(3):
                for l in range(L):
                    lanes = slice(128 * l, 128 * l + 128)
                    U[1, i, z + 2, l, body_rows, :] = U[1, i, z + 2, l, body_rows, :] + (
                        TZ[z + 2, i, :, lanes] - TZ[z, i, :, lanes]
                    )

        def finish_pool(z, row):
            means = []
            for i in range(3):
                value = moved_ref[i, z] + (TZ[z + 2, i] - TZ[z, i])
                moved_ref[i, z] = value
                folded = value[:, 0:128]
                for cut in range(128, C, 128):
                    folded = folded + value[:, cut:cut + 128]
                means.append(jnp.sum(folded, axis=1, keepdims=True) * (1.0 / C))
            pooled_t[row:row + R, :] = jnp.where(
                lane_r == 0, means[0], jnp.where(lane_r == 1, means[1], means[2])
            )

        def pooled(rows_here):
            value = pooled_t[0:rows_here, :].T[0:8].astype(jnp.bfloat16)
            return jnp.concatenate([value, value], axis=1)

        settle(2 * 3 * 2 * L * R // 8, in_sem.at[0])
        with scope("barrier"):
            pl.semaphore_wait(barrier, met)
        send(0, "zu")
        pack_corners(0)
        send(0, "zx", "zy")
        crack_load.wait()

        def label(z, carry):
            for l in range(L):
                U[0, 3, z + 2, l, body_rows, :] = DAMAGE_LEVEL * crack[
                    z, :, 128 * l:128 * l + 128
                ].astype(F32)
            return carry

        lax.fori_loop(0, Z, label, 0)
        settle(3 * (Z - 4) * L * R // 8, in_sem.at[4])
        with scope("pack"):
            pack_y(0, 0)
            send(0, "y0", "yx0", "x0", "zd", "zs")
            for item in [tough_load, *weight_loads]:
                item.start()
        for side, sign in ((0, -1), (1, 1)):
            clear((sign, 0, 0), clear_z(side))
            clear((0, sign, 0), clear_y(side))
            clear((0, 0, sign), clear_x(side))

        cell_load.wait()
        base = me[0] * Z * (R * n_pencil) + me[1] * R
        row_id = lax.broadcasted_iota(jnp.int32, (R, 512), 0) * n_comp

        def choose(part, z, row):
            start = (base + z * (R * n_pencil)) * n_comp + me[2]
            for s in range(0, sensors, 512):
                hit = row_id == cell_ref[:, s:s + 512] - start
                weight[part, row:row + R, s:s + 512] = jnp.where(hit, POINT_GAIN, 0.0).astype(
                    jnp.bfloat16
                )

        with scope("choose"):
            for k, z in enumerate((0, 1, Z - 2, Z - 1)):
                choose(0, z, rim + k * R)
            for z in range(2, Z - 2):
                choose(1, z, inner + (z - 2) * R)
            tough_load.wait()
        with scope("waitx"):
            receive(0, "x0")
        with scope("unpx"):
            loop(0, Z, lambda z: unpack_x(0, z))
        with scope("waity"):
            receive(0, "y0", "yx0")
        with scope("unpy"):
            loop(0, Z, lambda z: unpack_y(0, z, 4))
            unpack_yx(0, 0)
        with scope("body"):
            loop(0, 2, lambda k: force(0, 2 + k * (Z - 5), True))
            loop(0, 2, lambda k: force(0, 1 + k * (Z - 3), False))
        with scope("waitza"):
            receive(0, *EDGE)
        with scope("edge"):
            unpack_zx(0)
            for z in (-1, Z):
                unpack_y(0, z, 3)
            loop(0, 2, lambda k: force(0, k * (Z - 1), False))
            loop(0, 2, lambda k: finish(0, 1 + k * (Z - 3)))
        send(1, "zs")
        with scope("body2"):
            loop(3, Z - 3, lambda z: force(0, z, True))
            loop(2, Z - 2, lambda z: finish(0, z))
            pack_y(1, 0)
            send(1, "y0", "yx0", "x0")
            loop(0, 2, lambda k: damage(0, 1 + k * (Z - 3)))
        with scope("waitzb"):
            receive(0, *REST)
        with scope("ends"):
            loop(0, 2, lambda k: ends(0, k * (Z + 1) - 1))
            loop(0, 2, lambda k: finish(0, k * (Z - 1)))
        pack_corners(1)
        send(1, "zu", "zx", "zy")
        with scope("damage"):
            loop(0, 2, lambda k: damage(0, k * (Z - 1)))
        send(1, "zd")
        with scope("pack2"):
            pack_y(1, 1)
            send(1, "y1", "y2", "yx1", "x1", "x2")

        with scope("waitx"):
            receive(1, "x0")
            loop(2, Z - 2, lambda z: unpack_x(1, z))
        with scope("waity"):
            receive(1, "y0", "yx0")
            loop(2, Z - 2, lambda z: unpack_y(1, z, 4))
            unpack_yx(1, 0)
        with scope("body"):
            loop(3, Z - 3, lambda z: force(1, z, False))
        with scope("waitxy"):
            receive(1, "x1", "x2", "y1", "y2", "yx1")
        with scope("unpxy"):
            for z in (0, 1, Z - 2, Z - 1):
                unpack_x(1, z)
                unpack_y(1, z, 4)
            unpack_yx(1, 1)
        with scope("body2"):
            loop(0, 2, lambda k: force(1, 1 + k * (Z - 3), False))
            loop(0, 2, lambda k: force(1, 2 + k * (Z - 5), False))
        with scope("pooli"):
            for z in range(2, Z - 2):
                finish_pool(z, (z - 2) * R)
        with scope("doti"):
            settle(Z * R * sensors * 2 // 4096, in_sem.at[5])
            lhs = pooled(inner)
            for cut in range(0, sensors, 256):
                acc[:, cut:cut + 256] = jnp.dot(
                    lhs, weight[1, 0:2 * inner, cut:cut + 256], preferred_element_type=F32
                )
        with scope("waitz"):
            receive(1, *REST, *EDGE)
        with scope("edge"):
            unpack_zx(1)
            for z in (-1, Z):
                unpack_y(1, z, 3)
            loop(0, 2, lambda k: force(1, k * (Z - 1), False))
            loop(0, 2, lambda k: ends(1, k * (Z + 1) - 1))
        with scope("poole"):
            for k, z in enumerate((0, 1, Z - 2, Z - 1)):
                finish_pool(z, k * R)

        def spread(stop, function):
            if stop <= 16:
                for k in range(stop):
                    function(k)
            else:
                loop(0, stop, function)

        def owner(q):
            return {"slab": first_slab + q // n_pencil, "pencil": q % n_pencil, "comp": n_comp - 1}

        def owned_by(q):
            return jnp.logical_and(mine == q, me[2] == n_comp - 1)

        def scatter(q):
            return pltpu.make_async_remote_copy(
                src_ref=partial.at[q], dst_ref=RB.at[flat],
                send_sem=send_sem.at[1], recv_sem=recv_sem.at[8],
                device_id=owner(q), device_id_type=MESH,
            )

        def landed(ref, sem):
            pltpu.make_async_copy(ref, ref, sem).wait()

        def gather(q, k):
            return pltpu.make_async_remote_copy(
                src_ref=GB.at[q], dst_ref=GB.at[q],
                send_sem=send_sem.at[2], recv_sem=recv_sem.at[9],
                device_id=device(k), device_id_type=MESH,
            )

        def unless(same, function):
            @pl.when(jnp.logical_not(same))
            def _():
                function()

        mine = (me[0] - first_slab) * n_pencil + me[1]
        owning = jnp.logical_and(
            me[2] == n_comp - 1, jnp.logical_and(mine >= 0, mine < owners)
        )
        with scope("dot"):
            lhs = pooled(rim)
            for cut in range(0, sensors, 256):
                value = acc[:, cut:cut + 256] + jnp.dot(
                    lhs, weight[0, 0:2 * rim, cut:cut + 256], preferred_element_type=F32
                )
                for low in (0, 128):
                    for c in range(3):
                        partial[(cut + low) // piece, c, (cut + low) % piece // 128] = (
                            value[c, low:low + 128]
                        )
        with scope("rssend"):
            for q in range(owners):
                unless(owned_by(q), lambda: scatter(q).start())

        with scope("damage"):
            loop(0, Z, lambda z: damage(1, z))

        @pl.when(owning)
        def _():
            with scope("waitrs"):
                landed(RB.at[0:count - 1], recv_sem.at[8])
            RB[flat] = partial[mine]
            if count <= 16:
                total = RB[0]
                for k in range(1, count):
                    total = total + RB[k]
            else:
                total = lax.fori_loop(1, count, lambda k, t: t + RB[k], RB[0])
            GB[mine] = total
            spread(count, lambda k: unless(flat == k, lambda: gather(mine, k).start()))

        with scope("waitag"):
            @pl.when(owning)
            def _():
                if owners > 1:
                    landed(GB.at[0:owners - 1], recv_sem.at[9])

            @pl.when(jnp.logical_not(owning))
            def _():
                landed(GB.at[0:owners], recv_sem.at[9])

        for q in range(owners):
            for c in range(3):
                for k in range(strips):
                    low = q * piece + 128 * k
                    read_ref[c, low:low + 128] = GB[q, c, k]
        with scope("sends"):
            settle_messages((0, 1), lambda t: SENT[t], send_sem.at[0])

            @pl.when(owning)
            def _():
                if owners > 1:
                    landed(partial.at[0:owners - 1], send_sem.at[1])
                landed(RB.at[0:count - 1], send_sem.at[2])

            @pl.when(jnp.logical_not(owning))
            def _():
                landed(partial.at[0:owners], send_sem.at[1])

    return kernel


def emit(moved_ref, damage_ref, read_ref, moved_hbm, damage_hbm, read_hbm, sem):
    copies = [
        pltpu.make_async_copy(moved_ref, moved_hbm, sem.at[0]),
        pltpu.make_async_copy(damage_ref, damage_hbm, sem.at[1]),
        pltpu.make_async_copy(read_ref, read_hbm, sem.at[2]),
    ]
    for copy in copies:
        copy.start()
    for copy in copies:
        copy.wait()


def solution(mesh):
    sizes = tuple(mesh.shape[a] for a in AXES)
    n_slab = sizes[0]
    count = sizes[0] * sizes[1] * sizes[2]

    def local(u_start, toughness, crack_label, obs_weight, sensor_cell):
        Z, R, C = toughness.shape
        S = sensor_cell.shape[0]
        first_slab = max(n_slab // 2 - 1, 0)
        owners = min(2, n_slab) * sizes[1]
        while S % (owners * 256):
            owners -= 1
        piece = S // owners
        rim, inner = 4 * R, (Z - 4) * R
        most = max(
            Z * R * S * 2 // 4096,
            sum(group_tiles(t, SENT[t], (2, 2, 2), Z, R, C // 128) for t in range(2)),
        )
        any_spec = pl.BlockSpec(memory_space=pltpu.HBM)
        vmem_spec = pl.BlockSpec(memory_space=pltpu.VMEM)
        dma = pltpu.SemaphoreType.DMA
        shapes = (
            jax.ShapeDtypeStruct((3, Z, R, C), F32),
            jax.ShapeDtypeStruct((Z, R, C), F32),
            jax.ShapeDtypeStruct((3, S), F32),
        )
        outs = pl.pallas_call(
            make_kernel(Z, R, C, S, sizes, first_slab, owners),
            out_shape=shapes,
            in_specs=[any_spec] * 5,
            out_specs=[vmem_spec] * 3,
            scratch_shapes=[
                pltpu.VMEM((2, 4, Z + 4, C // 128 + 1, R + 32, 128), F32),
                pltpu.VMEM((2, 2, 4, Z, R, 128), F32),
                pltpu.VMEM((2, 2, 2, R, 128), F32),
                pltpu.VMEM((2, 2, 2, R, 128), F32),
                pltpu.VMEM((2, 2, Z + 2, 8, C), F32),
                pltpu.VMEM((2, 2, Z, 8, C), F32),
                pltpu.VMEM((2, 2, 2, 8, C), F32),
                pltpu.VMEM((2, 2, 2, 2, 8, 128), F32),
                pltpu.VMEM((2, 2, 2, 2, 8, 128), F32),
                pltpu.VMEM((Z + 2, 3, R, C), F32),
                pltpu.VMEM((3, C // 128, R + 32, 128), F32),
                pltpu.VMEM((most, 8, 128), F32),
                pltpu.VMEM((Z, R, C), F32),
                pltpu.VMEM((Z, R, C), jnp.int32),
                pltpu.VMEM((2, 2 * max(rim, inner), S), jnp.bfloat16),
                pltpu.VMEM((1, S), jnp.int32),
                pltpu.VMEM((max(rim, inner), 128), F32),
                pltpu.VMEM((8, S), F32),
                pltpu.VMEM((owners, 3, piece // 128, 128), F32),
                pltpu.VMEM((count, 3, piece // 128, 128), F32),
                pltpu.VMEM((owners, 3, piece // 128, 128), F32),
                dma((6,)),
                dma((3,)),
                dma((10,)),
            ],
            compiler_params=pltpu.CompilerParams(
                collective_id=0, has_side_effects=True, vmem_limit_bytes=40 * 1024 * 1024
            ),
            name="fracture",
        )(
            *[
                pltpu.with_memory_space_constraint(x, pltpu.HBM)
                for x in (
                    u_start, toughness, crack_label, obs_weight.reshape(Z * R, S),
                    sensor_cell.reshape(1, S),
                )
            ],
        )
        return pl.pallas_call(
            emit,
            out_shape=shapes,
            in_specs=[vmem_spec] * 3,
            out_specs=[any_spec] * 3,
            scratch_shapes=[dma((3,))],
            name="emit",
        )(*[pltpu.with_memory_space_constraint(x, pltpu.VMEM) for x in outs])

    return jax.shard_map(
        local,
        mesh=mesh,
        in_specs=(
            P(None, ("groups", "slab"), "pencil", "comp"),
            P(("groups", "slab"), "pencil", "comp"),
            P(("groups", "slab"), "pencil", "comp"),
            P("slab", "pencil", "comp", None),
            P(),
        ),
        out_specs=(
            P(None, ("groups", "slab"), "pencil", "comp"),
            P(("groups", "slab"), "pencil", "comp"),
            P(None, "groups"),
        ),
        check_vma=False,
    )
```

time: 32.1 us -> 28.7 us (0.89)
  Pallas kernels: 31.3 us -> 27.9 us
    pallas_call x1, Pallas kernels: 30.3 us -> 26.9 us  [local(): pl.pallas_call(make_kernel(Z, R, C, S, sizes, first_slab, owners), out_sh...]
where the time goes in v2:
time: 28.7 us; the launch traced here: 28.6 us
  Pallas kernels  27.9 us (97%)
  between operations  0.64 us (2%)
    pallas_call x1, Pallas kernels, local(): pl.pallas_call(make_kernel(Z, R, C, S, sizes, first_slab, owners), out_sh...  26.9 us
    pallas_call x1, Pallas kernels, local(): pl.pallas_call(emit, out_shape=shapes, in_specs=[vmem_spec] * 3, out_spec...  1 us

profile of v2, /device:TPU:0, one launch (start us, length us, event | category | flops | bytes accessed | tf_op | source)
XLA Modules:
  0.0 28.6 jit_solution(3949005091392560740)
XLA Ops:
  0.6 26.9 %fracture.1 = (f32[3,8,32,256]{3,2,1,0:T(8,128)S(1)}, f32[8,32,256]{2,1,0:T(8,128)S(1)}, f32[3,4096]{1,0:T(4,128)S(1)}) custom-call(f32[3,8,32,256]{3,2,1,0:T(8,128)} %u_hbm.1, f32[8,32,256]{2,1,0:T(8,128)} %tough_hbm.1, s32[8,32,256]{2,1,0:T(8,128)} %crack_hbm.1, bf16[256,4096]{1,0:T(8,128)(2,1)} %bitcast.2, s32[1,4096]{1,0:T(1,128)} %bitcast.3), custom_call_target="tpu_custom_call" | custom-call | tf_op jit(solution)/shard_map/fracture/pallas_call | solution.py:852
  27.5 1.0 %emit.1 = (f32[3,8,32,256]{3,2,1,0:T(8,128)}, f32[8,32,256]{2,1,0:T(8,128)}, f32[3,4096]{1,0:T(4,128)}) custom-call(f32[3,8,32,256]{3,2,1,0:T(8,128)S(1)} %get-tuple-element.6.moved_ref, f32[8,32,256]{2,1,0:T(8,128)S(1)} %get-tuple-element.7.damage_ref, f32[3,4096]{1,0:T(4,128)S(1)} %get-tuple-element.8.read_ref), custom_call_target="tpu_custom_call" | custom-call | tf_op jit(solution)/shard_map/emit/pallas_call | solution.py:896

commit v3 on v2

--- a/solution.py
+++ b/solution.py
@@ -80,12 +80,12 @@
     if kind == "zd":
         return L * R // 8
     if kind == "zx":
-        return R // 8
+        return 1
     if kind == "zy":
         return L
     if kind[:2] == "yx":
         return 1
-    planes = 2 if kind[1] != "0" else Z - 4 if step else Z
+    planes = 1 if kind[1] != "0" else Z - 2 if step else Z
     return planes * L if kind[0] == "y" else planes * 4 * R // 8
 
 
@@ -119,9 +119,9 @@
     rim = 4 * R
     spans = {
         0: {"0": (0, Z)},
-        1: {"0": (2, Z - 2), "1": (0, 2), "2": (Z - 2, Z)},
+        1: {"0": (1, Z - 1), "1": (0, 1), "2": (Z - 1, Z)},
     }
-    groups = {0: [range(Z)], 1: [range(2, Z - 2), [0, 1, Z - 2, Z - 1]]}
+    groups = {0: [range(Z)], 1: [range(1, Z - 1), [0, Z - 1]]}
     near = n_slab <= 4 and n_pencil <= 2 and n_comp <= 2
 
     def scope(name):
@@ -165,7 +165,7 @@
             pltpu.make_async_copy(
                 weight_hbm.at[rim // 2:Z * R - rim // 2], weight.at[1, 0:inner], in_sem.at[5]),
         ]
-        for item in [*edge_loads, crack_load, *inner_loads, cell_load]:
+        for item in edge_loads:
             item.start()
 
         barrier = pltpu.get_barrier_semaphore()
@@ -205,6 +205,9 @@
             lax.fori_loop(1, count, greet, 0)
             met = count - 1
 
+        for item in [crack_load, *inner_loads, cell_load]:
+            item.start()
+
         def clear(d, write):
             if feasible(d):
                 @pl.when(jnp.logical_not(inside(d, 1)))
@@ -218,7 +221,7 @@
                 for step in range(2):
                     for z in ((Z + 2, Z + 3) if up else (0, 1)):
                         U[step, :, z, 0:L, body_rows] = jnp.zeros((4, L, R, 128), F32)
-                XC[:, up] = jnp.zeros((2, 2, R, 128), F32)
+                XC[:, up] = jnp.zeros((2, 2, 8, 128), F32)
                 for step in range(2):
                     for side in range(2):
                         YR[step, side, (Z + 1) * up] = jnp.zeros((8, C), F32)
@@ -231,7 +234,7 @@
                     return carry
 
                 lax.fori_loop(0, 8 * Z, one, 0)
-                XC[:, :, right] = jnp.zeros((2, 2, R, 128), F32)
+                XC[:, :, right] = jnp.zeros((2, 2, 8, 128), F32)
                 YXR[:, :, right] = jnp.zeros((2, 2, 2, 8, 128), F32)
             return write
 
@@ -241,6 +244,7 @@
                 YXR[:, up] = jnp.zeros((2, 2, 2, 8, 128), F32)
             return write
 
+        core_rows = range(TOP, END, 8)
         row8t = lax.broadcasted_iota(jnp.int32, (8, 128), 0)
         lane8 = lax.broadcasted_iota(jnp.int32, (8, 128), 1)
         lane_r = lax.broadcasted_iota(jnp.int32, (R, 128), 1)
@@ -261,7 +265,9 @@
                 return 0 if kind in EDGE else 1 if kind in REST else 2 if kind[0] == "x" else 3
             if kind[0] == "z":
                 return 4
-            return 7 if kind[-1] != "0" else 5 if kind[0] == "x" else 6
+            if kind[-1] == "0":
+                return 5 if kind[0] == "x" else 6
+            return 10 if kind[0] == "x" else 7
 
         def message(step, kind, d):
             dz, dy, dx = d
@@ -372,13 +378,13 @@
         def pack_corners(step):
             for sz, z in ((0, 0), (1, Z - 1)):
                 for sx in range(2):
-                    tiles = [
-                        roll(U[step, f, z + 2, (L - 1) * sx, body_rows, :], f + sx, 1)
-                        for f in range(3)
-                    ]
-                    XS[step, sz, sx] = jnp.where(
-                        lane_r == 0, tiles[0], jnp.where(lane_r == 1, tiles[1], tiles[2])
-                    )
+                    tile = jnp.zeros((8, 128), F32)
+                    for k, row in enumerate(core_rows):
+                        for f in range(3):
+                            value = U[step, f, z + 2, (L - 1) * sx, row:row + 8, :]
+                            lane = 3 * k + f
+                            tile = jnp.where(lane8 == lane, roll(value, lane + sx, 1), tile)
+                    XS[step, sz, sx] = tile
 
                 def save(side, l, value):
                     YZ[step, side, sz, :, 128 * l:128 * l + 128] = value
@@ -393,10 +399,13 @@
 
         def unpack_zx(step):
             for sz, z in ((0, -1), (1, Z)):
-                for f in range(3):
-                    U[step, f, z + 2, L, body_rows, :] = jnp.where(
-                        lane_r < 64, roll(XC[step, sz, 1], -f, 1), roll(XC[step, sz, 0], 127 - f, 1)
-                    )
+                right, left = XC[step, sz, 1], XC[step, sz, 0]
+                for k, row in enumerate(core_rows):
+                    for f in range(3):
+                        lane = 3 * k + f
+                        U[step, f, z + 2, L, row:row + 8, :] = jnp.where(
+                            lane8 < 64, roll(right, -lane, 1), roll(left, 127 - lane, 1)
+                        )
 
         def put_rows(step, z, l, low, high, fields):
             for f in range(fields):
@@ -460,8 +469,6 @@
                 moved_ref[f, z, row - TOP:row - TOP + 8, :] = value
             else:
                 damage_ref[z, row - TOP:row - TOP + 8, :] = value
-
-        core_rows = range(TOP, END, 8)
 
         def ends(step, z):
             for row in core_rows:
@@ -500,62 +507,85 @@
                     gz[1] + gy[0], gz[2] + gx[0], gy[2] + gx[1],
                 )
 
-        def put_y(row, values):
+        def put_y(z, row, values):
             for i in range(3):
                 for l in range(L):
-                    TY[i, l, row:row + 8, :] = values[i][:, 128 * l:128 * l + 128]
-
-        def force(step, z, with_damage):
+                    TY[z, i, l, row:row + 8, :] = values[i][:, 128 * l:128 * l + 128]
+
+        def outer_rows(step, z):
             for row in (TOP - 8, END):
                 gy = [slope_y(step, f, z, row, L) for f in range(3)]
                 gx1, gx2 = [slope_x(step, f, z, row) for f in (1, 2)]
                 gz0, gz1 = [slope_z(step, f, z, row, L) for f in (0, 1)]
                 g = gain(step, z, row, L)
                 h = 0.5 * g
-                put_y(row, [
+                put_y(z, row, [
                     h * (gz1 + gy[0]), g * (gy[1] + 0.75 * (gz0 + gy[1] + gx2)), h * (gy[2] + gx1)
                 ])
 
-            def close(row, waiting):
-                for i in range(3):
-                    change = jnp.concatenate(
-                        [TY[i, l, row + 1:row + 9, :] - TY[i, l, row - 1:row + 7, :] for l in range(L)],
-                        axis=1,
-                    )
-                    store(step, i, z, row, waiting[i] + change)
-
+        def close(step, z, row, waiting):
+            for i in range(3):
+                change = jnp.concatenate(
+                    [TY[z, i, l, row + 1:row + 9, :] - TY[z, i, l, row - 1:row + 7, :] for l in range(L)],
+                    axis=1,
+                )
+                store(step, i, z, row, waiting[i] + change)
+
+        def held(step, i, z, row):
+            if step:
+                return moved_ref[i, z, row - TOP:row - TOP + 8, :]
+            return take(1, i, z + 2, row, L)
+
+        def strip(step, z, row, with_damage):
+            wide = L + 1
+            now = [take(step, f, z + 2, row, wide) for f in range(3)]
+            gz = [slope_z(step, f, z, row, wide) for f in range(3)]
+            gy = [slope_y(step, f, z, row, wide) for f in range(3)]
+            gx = [along_x(v, wide) for v in now]
+            g = gain(step, z, row, wide)
+            h = 0.5 * g
+            lam = 0.75 * (gz[0] + gy[1] + gx[2])
+            a01 = (gz[1] + gy[0])[:, 0:C]
+            a02 = gz[2] + gx[0]
+            a12 = gy[2] + gx[1]
+            t01, t02, t12 = h[:, 0:C] * a01, h * a02, h * a12
+            put_y(z, row, [t01, (g * (gy[1] + lam))[:, 0:C], t12[:, 0:C]])
+            at = slice(row - TOP, row - TOP + 8)
+            TZ[z + 1, 0, at] = (g * (gz[0] + lam))[:, 0:C]
+            TZ[z + 1, 1, at] = t01
+            TZ[z + 1, 2, at] = t02[:, 0:C]
+            if with_damage:
+                hurt(
+                    step, z, row, gz[0][:, 0:C], gy[1][:, 0:C], gx[2][:, 0:C],
+                    a01, a02[:, 0:C], a12[:, 0:C],
+                )
+            return [
+                now[i][:, 0:C] + along_x(t, L) for i, t in enumerate((t02, t12, g * (gx[2] + lam)))
+            ]
+
+        def force_mid(step, z, with_damage):
+            for row in core_rows[1:-1]:
+                for i, value in enumerate(strip(step, z, row, with_damage)):
+                    store(step, i, z, row, value)
+
+        def force_rim(step, z, with_damage):
+            outer_rows(step, z)
+            first = strip(step, z, core_rows[0], with_damage)
+            last = strip(step, z, core_rows[-1], with_damage)
+            close(step, z, core_rows[0], first)
+            for row in core_rows[1:-1]:
+                close(step, z, row, [held(step, i, z, row) for i in range(3)])
+            close(step, z, core_rows[-1], last)
+
+        def force(step, z):
+            outer_rows(step, z)
             waiting = None
             for row in core_rows:
-                wide = L + 1
-                now = [take(step, f, z + 2, row, wide) for f in range(3)]
-                gz = [slope_z(step, f, z, row, wide) for f in range(3)]
-                gy = [slope_y(step, f, z, row, wide) for f in range(3)]
-                gx = [along_x(v, wide) for v in now]
-                g = gain(step, z, row, wide)
-                h = 0.5 * g
-                lam = 0.75 * (gz[0] + gy[1] + gx[2])
-                a01 = (gz[1] + gy[0])[:, 0:C]
-                a02 = gz[2] + gx[0]
-                a12 = gy[2] + gx[1]
-                t01, t02, t12 = h[:, 0:C] * a01, h * a02, h * a12
-                put_y(row, [t01, (g * (gy[1] + lam))[:, 0:C], t12[:, 0:C]])
-                at = slice(row - TOP, row - TOP + 8)
-                TZ[z + 1, 0, at] = (g * (gz[0] + lam))[:, 0:C]
-                TZ[z + 1, 1, at] = t01
-                TZ[z + 1, 2, at] = t02[:, 0:C]
-                ready = [
-                    now[i][:, 0:C] + along_x(t, L)
-                    for i, t in enumerate((t02, t12, g * (gx[2] + lam)))
-                ]
+                ready = strip(step, z, row, False)
                 if waiting is not None:
-                    close(row - 8, waiting)
+                    close(step, z, row - 8, waiting)
                 waiting = ready
-                if with_damage:
-                    hurt(
-                        step, z, row, gz[0][:, 0:C], gy[1][:, 0:C], gx[2][:, 0:C],
-                        a01, a02[:, 0:C], a12[:, 0:C],
-                    )
-            close(END - 8, waiting)
+            close(step, z, END - 8, waiting)
 
         def finish(step, z):
             for i in range(3):
@@ -601,7 +631,7 @@
         settle(3 * (Z - 4) * L * R // 8, in_sem.at[4])
         with scope("pack"):
             pack_y(0, 0)
-            send(0, "y0", "yx0", "x0", "zd", "zs")
+            send(0, "y0", "yx0", "x0")
             for item in [tough_load, *weight_loads]:
                 item.start()
         for side, sign in ((0, -1), (1, 1)):
@@ -627,33 +657,36 @@
             for z in range(2, Z - 2):
                 choose(1, z, inner + (z - 2) * R)
             tough_load.wait()
+        send(0, "zd", "zs")
         with scope("waitx"):
             receive(0, "x0")
         with scope("unpx"):
             loop(0, Z, lambda z: unpack_x(0, z))
+        with scope("mid"):
+            loop(1, Z - 1, lambda z: force_mid(0, z, True))
         with scope("waity"):
             receive(0, "y0", "yx0")
         with scope("unpy"):
             loop(0, Z, lambda z: unpack_y(0, z, 4))
             unpack_yx(0, 0)
         with scope("body"):
-            loop(0, 2, lambda k: force(0, 2 + k * (Z - 5), True))
-            loop(0, 2, lambda k: force(0, 1 + k * (Z - 3), False))
+            loop(0, 2, lambda k: force_rim(0, 2 + k * (Z - 5), True))
+            loop(0, 2, lambda k: force_rim(0, 1 + k * (Z - 3), True))
         with scope("waitza"):
             receive(0, *EDGE)
         with scope("edge"):
             unpack_zx(0)
             for z in (-1, Z):
                 unpack_y(0, z, 3)
-            loop(0, 2, lambda k: force(0, k * (Z - 1), False))
+            loop(0, 2, lambda k: ends(0, k * (Z - 1)))
             loop(0, 2, lambda k: finish(0, 1 + k * (Z - 3)))
         send(1, "zs")
         with scope("body2"):
-            loop(3, Z - 3, lambda z: force(0, z, True))
+            loop(3, Z - 3, lambda z: force_rim(0, z, True))
             loop(2, Z - 2, lambda z: finish(0, z))
+            loop(0, 2, lambda k: force(0, k * (Z - 1)))
             pack_y(1, 0)
             send(1, "y0", "yx0", "x0")
-            loop(0, 2, lambda k: damage(0, 1 + k * (Z - 3)))
         with scope("waitzb"):
             receive(0, *REST)
         with scope("ends"):
@@ -670,23 +703,28 @@
 
         with scope("waitx"):
             receive(1, "x0")
-            loop(2, Z - 2, lambda z: unpack_x(1, z))
+            loop(1, Z - 1, lambda z: unpack_x(1, z))
+        with scope("mid"):
+            loop(2, Z - 2, lambda z: force_mid(1, z, False))
+        with scope("waitxe"):
+            receive(1, "x1", "x2")
+        with scope("mide"):
+            for z in (0, Z - 1):
+                unpack_x(1, z)
+            loop(0, 2, lambda k: force_mid(1, 1 + k * (Z - 3), False))
         with scope("waity"):
             receive(1, "y0", "yx0")
-            loop(2, Z - 2, lambda z: unpack_y(1, z, 4))
+            loop(1, Z - 1, lambda z: unpack_y(1, z, 4))
             unpack_yx(1, 0)
-        with scope("body"):
-            loop(3, Z - 3, lambda z: force(1, z, False))
-        with scope("waitxy"):
-            receive(1, "x1", "x2", "y1", "y2", "yx1")
-        with scope("unpxy"):
-            for z in (0, 1, Z - 2, Z - 1):
-                unpack_x(1, z)
+        with scope("rim"):
+            loop(2, Z - 2, lambda z: force_rim(1, z, False))
+        with scope("waitye"):
+            receive(1, "y1", "y2", "yx1")
+        with scope("rime"):
+            for z in (0, Z - 1):
                 unpack_y(1, z, 4)
             unpack_yx(1, 1)
-        with scope("body2"):
-            loop(0, 2, lambda k: force(1, 1 + k * (Z - 3), False))
-            loop(0, 2, lambda k: force(1, 2 + k * (Z - 5), False))
+            loop(0, 2, lambda k: force_rim(1, 1 + k * (Z - 3), False))
         with scope("pooli"):
             for z in range(2, Z - 2):
                 finish_pool(z, (z - 2) * R)
@@ -703,7 +741,7 @@
             unpack_zx(1)
             for z in (-1, Z):
                 unpack_y(1, z, 3)
-            loop(0, 2, lambda k: force(1, k * (Z - 1), False))
+            loop(0, 2, lambda k: force(1, k * (Z - 1)))
             loop(0, 2, lambda k: ends(1, k * (Z + 1) - 1))
         with scope("poole"):
             for k, z in enumerate((0, 1, Z - 2, Z - 1)):
@@ -857,15 +895,15 @@
             scratch_shapes=[
                 pltpu.VMEM((2, 4, Z + 4, C // 128 + 1, R + 32, 128), F32),
                 pltpu.VMEM((2, 2, 4, Z, R, 128), F32),
-                pltpu.VMEM((2, 2, 2, R, 128), F32),
-                pltpu.VMEM((2, 2, 2, R, 128), F32),
+                pltpu.VMEM((2, 2, 2, 8, 128), F32),
+                pltpu.VMEM((2, 2, 2, 8, 128), F32),
                 pltpu.VMEM((2, 2, Z + 2, 8, C), F32),
                 pltpu.VMEM((2, 2, Z, 8, C), F32),
                 pltpu.VMEM((2, 2, 2, 8, C), F32),
                 pltpu.VMEM((2, 2, 2, 2, 8, 128), F32),
                 pltpu.VMEM((2, 2, 2, 2, 8, 128), F32),
                 pltpu.VMEM((Z + 2, 3, R, C), F32),
-                pltpu.VMEM((3, C // 128, R + 32, 128), F32),
+                pltpu.VMEM((Z, 3, C // 128, R + 32, 128), F32),
                 pltpu.VMEM((most, 8, 128), F32),
                 pltpu.VMEM((Z, R, C), F32),
                 pltpu.VMEM((Z, R, C), jnp.int32),
@@ -878,7 +916,7 @@
                 pltpu.VMEM((owners, 3, piece // 128, 128), F32),
                 dma((6,)),
                 dma((3,)),
-                dma((10,)),
+                dma((11,)),
             ],
             compiler_params=pltpu.CompilerParams(
                 collective_id=0, has_side_effects=True, vmem_limit_bytes=40 * 1024 * 1024

time: 28.7 us -> 27.4 us (0.955)
  Pallas kernels: 27.9 us -> 26.6 us
    pallas_call x1, Pallas kernels: 26.9 us -> 25.6 us  [local(): pl.pallas_call(make_kernel(Z, R, C, S, sizes, first_slab, owners), out_sh...]
where the time goes in v3:
time: 27.4 us; the launch traced here: 27.2 us
  Pallas kernels  26.6 us (97%)
  between operations  0.64 us (2%)
    pallas_call x1, Pallas kernels, local(): pl.pallas_call(make_kernel(Z, R, C, S, sizes, first_slab, owners), out_sh...  25.6 us
    pallas_call x1, Pallas kernels, local(): pl.pallas_call(emit, out_shape=shapes, in_specs=[vmem_spec] * 3, out_spec...  1 us

profile of v3, /device:TPU:0, one launch (start us, length us, event | category | flops | bytes accessed | tf_op | source)
XLA Modules:
  0.0 27.2 jit_solution(7421868847846635470)
XLA Ops:
  0.6 25.6 %fracture.1 = (f32[3,8,32,256]{3,2,1,0:T(8,128)S(1)}, f32[8,32,256]{2,1,0:T(8,128)S(1)}, f32[3,4096]{1,0:T(4,128)S(1)}) custom-call(f32[3,8,32,256]{3,2,1,0:T(8,128)} %u_hbm.1, f32[8,32,256]{2,1,0:T(8,128)} %tough_hbm.1, s32[8,32,256]{2,1,0:T(8,128)} %crack_hbm.1, bf16[256,4096]{1,0:T(8,128)(2,1)} %bitcast.2, s32[1,4096]{1,0:T(1,128)} %bitcast.3), custom_call_target="tpu_custom_call" | custom-call | tf_op jit(solution)/shard_map/fracture/pallas_call | solution.py:890
  26.2 1.0 %emit.1 = (f32[3,8,32,256]{3,2,1,0:T(8,128)}, f32[8,32,256]{2,1,0:T(8,128)}, f32[3,4096]{1,0:T(4,128)}) custom-call(f32[3,8,32,256]{3,2,1,0:T(8,128)S(1)} %get-tuple-element.6.moved_ref, f32[8,32,256]{2,1,0:T(8,128)S(1)} %get-tuple-element.7.damage_ref, f32[3,4096]{1,0:T(4,128)S(1)} %get-tuple-element.8.read_ref), custom_call_target="tpu_custom_call" | custom-call | tf_op jit(solution)/shard_map/emit/pallas_call | solution.py:934

commit v4 on v3

--- a/solution.py
+++ b/solution.py
@@ -512,16 +512,17 @@
                 for l in range(L):
                     TY[z, i, l, row:row + 8, :] = values[i][:, 128 * l:128 * l + 128]
 
-        def outer_rows(step, z):
+        def outer_rows(step, z, flat=False):
             for row in (TOP - 8, END):
                 gy = [slope_y(step, f, z, row, L) for f in range(3)]
                 gx1, gx2 = [slope_x(step, f, z, row) for f in (1, 2)]
-                gz0, gz1 = [slope_z(step, f, z, row, L) for f in (0, 1)]
                 g = gain(step, z, row, L)
                 h = 0.5 * g
-                put_y(z, row, [
-                    h * (gz1 + gy[0]), g * (gy[1] + 0.75 * (gz0 + gy[1] + gx2)), h * (gy[2] + gx1)
-                ])
+                a01, trace = gy[0], gy[1] + gx2
+                if not flat:
+                    a01 = a01 + slope_z(step, 1, z, row, L)
+                    trace = trace + slope_z(step, 0, z, row, L)
+                put_y(z, row, [h * a01, g * (gy[1] + 0.75 * trace), h * (gy[2] + gx1)])
 
         def close(step, z, row, waiting):
             for i in range(3):
@@ -536,22 +537,27 @@
                 return moved_ref[i, z, row - TOP:row - TOP + 8, :]
             return take(1, i, z + 2, row, L)
 
-        def strip(step, z, row, with_damage):
+        def strip(step, z, row, with_damage, flat=False):
             wide = L + 1
             now = [take(step, f, z + 2, row, wide) for f in range(3)]
-            gz = [slope_z(step, f, z, row, wide) for f in range(3)]
             gy = [slope_y(step, f, z, row, wide) for f in range(3)]
             gx = [along_x(v, wide) for v in now]
             g = gain(step, z, row, wide)
             h = 0.5 * g
-            lam = 0.75 * (gz[0] + gy[1] + gx[2])
-            a01 = (gz[1] + gy[0])[:, 0:C]
-            a02 = gz[2] + gx[0]
+            trace = gy[1] + gx[2]
+            a01 = gy[0][:, 0:C]
+            a02 = gx[0]
+            if not flat:
+                gz = [slope_z(step, f, z, row, wide) for f in range(3)]
+                trace = trace + gz[0]
+                a01 = a01 + gz[1][:, 0:C]
+                a02 = a02 + gz[2]
+            lam = 0.75 * trace
             a12 = gy[2] + gx[1]
             t01, t02, t12 = h[:, 0:C] * a01, h * a02, h * a12
             put_y(z, row, [t01, (g * (gy[1] + lam))[:, 0:C], t12[:, 0:C]])
             at = slice(row - TOP, row - TOP + 8)
-            TZ[z + 1, 0, at] = (g * (gz[0] + lam))[:, 0:C]
+            TZ[z + 1, 0, at] = (g * (lam if flat else gz[0] + lam))[:, 0:C]
             TZ[z + 1, 1, at] = t01
             TZ[z + 1, 2, at] = t02[:, 0:C]
             if with_damage:
@@ -563,15 +569,15 @@
                 now[i][:, 0:C] + along_x(t, L) for i, t in enumerate((t02, t12, g * (gx[2] + lam)))
             ]
 
-        def force_mid(step, z, with_damage):
+        def force_mid(step, z, with_damage, flat=False):
             for row in core_rows[1:-1]:
-                for i, value in enumerate(strip(step, z, row, with_damage)):
+                for i, value in enumerate(strip(step, z, row, with_damage, flat)):
                     store(step, i, z, row, value)
 
-        def force_rim(step, z, with_damage):
-            outer_rows(step, z)
-            first = strip(step, z, core_rows[0], with_damage)
-            last = strip(step, z, core_rows[-1], with_damage)
+        def force_rim(step, z, with_damage, flat=False):
+            outer_rows(step, z, flat)
+            first = strip(step, z, core_rows[0], with_damage, flat)
+            last = strip(step, z, core_rows[-1], with_damage, flat)
             close(step, z, core_rows[0], first)
             for row in core_rows[1:-1]:
                 close(step, z, row, [held(step, i, z, row) for i in range(3)])
@@ -586,6 +592,54 @@
                     close(step, z, row - 8, waiting)
                 waiting = ready
             close(step, z, END - 8, waiting)
+
+        def add_z(z):
+            def put(row, first, second):
+                for l in range(L):
+                    lanes = slice(128 * l, 128 * l + 128)
+                    TY[z, 0, l, row:row + 8, :] = first[:, lanes]
+                    TY[z, 1, l, row:row + 8, :] = second[:, lanes]
+
+            def close_two(row, waiting):
+                at = slice(row - TOP, row - TOP + 8)
+                for i in range(3):
+                    value = moved_ref[i, z, at, :]
+                    if i != 1:
+                        value = value + waiting[i // 2]
+                    if i < 2:
+                        value = value + jnp.concatenate(
+                            [
+                                TY[z, i, l, row + 1:row + 9, :] - TY[z, i, l, row - 1:row + 7, :]
+                                for l in range(L)
+                            ],
+                            axis=1,
+                        )
+                    moved_ref[i, z, at, :] = value
+
+            for row in (TOP - 8, END):
+                g = gain(1, z, row, L)
+                put(
+                    row, (0.5 * g) * slope_z(1, 1, z, row, L),
+                    (0.75 * g) * slope_z(1, 0, z, row, L),
+                )
+            waiting = None
+            for row in core_rows:
+                at = slice(row - TOP, row - TOP + 8)
+                g = gain(1, z, row, L + 1)
+                h = 0.5 * g
+                p = g * slope_z(1, 0, z, row, L + 1)
+                q1 = h[:, 0:C] * slope_z(1, 1, z, row, L)
+                q2 = h * slope_z(1, 2, z, row, L + 1)
+                lam = 0.75 * p
+                put(row, q1, lam[:, 0:C])
+                TZ[z + 1, 0, at] = TZ[z + 1, 0, at] + (p + lam)[:, 0:C]
+                TZ[z + 1, 1, at] = TZ[z + 1, 1, at] + q1
+                TZ[z + 1, 2, at] = TZ[z + 1, 2, at] + q2[:, 0:C]
+                ready = [along_x(q2, L), along_x(lam, L)]
+                if waiting is not None:
+                    close_two(row - 8, waiting)
+                waiting = ready
+            close_two(END - 8, waiting)
 
         def finish(step, z):
             for i in range(3):
@@ -616,8 +670,6 @@
         with scope("barrier"):
             pl.semaphore_wait(barrier, met)
         send(0, "zu")
-        pack_corners(0)
-        send(0, "zx", "zy")
         crack_load.wait()
 
         def label(z, carry):
@@ -632,6 +684,8 @@
         with scope("pack"):
             pack_y(0, 0)
             send(0, "y0", "yx0", "x0")
+            pack_corners(0)
+            send(0, "zx", "zy")
             for item in [tough_load, *weight_loads]:
                 item.start()
         for side, sign in ((0, -1), (1, 1)):
@@ -675,12 +729,12 @@
         with scope("waitza"):
             receive(0, *EDGE)
         with scope("edge"):
-            unpack_zx(0)
-            for z in (-1, Z):
-                unpack_y(0, z, 3)
             loop(0, 2, lambda k: ends(0, k * (Z - 1)))
             loop(0, 2, lambda k: finish(0, 1 + k * (Z - 3)))
         send(1, "zs")
+        unpack_zx(0)
+        for z in (-1, Z):
+            unpack_y(0, z, 3)
         with scope("body2"):
             loop(3, Z - 3, lambda z: force_rim(0, z, True))
             loop(2, Z - 2, lambda z: finish(0, z))
@@ -712,6 +766,7 @@
             for z in (0, Z - 1):
                 unpack_x(1, z)
             loop(0, 2, lambda k: force_mid(1, 1 + k * (Z - 3), False))
+            loop(0, 2, lambda k: force_mid(1, k * (Z - 1), False, True))
         with scope("waity"):
             receive(1, "y0", "yx0")
             loop(1, Z - 1, lambda z: unpack_y(1, z, 4))
@@ -735,14 +790,17 @@
                 acc[:, cut:cut + 256] = jnp.dot(
                     lhs, weight[1, 0:2 * inner, cut:cut + 256], preferred_element_type=F32
                 )
+        with scope("flat"):
+            loop(0, 2, lambda k: force_rim(1, k * (Z - 1), False, True))
         with scope("waitz"):
             receive(1, *REST, *EDGE)
         with scope("edge"):
             unpack_zx(1)
             for z in (-1, Z):
                 unpack_y(1, z, 3)
-            loop(0, 2, lambda k: force(1, k * (Z - 1)))
-            loop(0, 2, lambda k: ends(1, k * (Z + 1) - 1))
+            for k in range(2):
+                ends(1, k * (Z + 1) - 1)
+                add_z(k * (Z - 1))
         with scope("poole"):
             for k, z in enumerate((0, 1, Z - 2, Z - 1)):
                 finish_pool(z, k * R)
@@ -850,15 +908,17 @@
 
 
 def emit(moved_ref, damage_ref, read_ref, moved_hbm, damage_hbm, read_hbm, sem):
-    copies = [
-        pltpu.make_async_copy(moved_ref, moved_hbm, sem.at[0]),
-        pltpu.make_async_copy(damage_ref, damage_hbm, sem.at[1]),
-        pltpu.make_async_copy(read_ref, read_hbm, sem.at[2]),
-    ]
-    for copy in copies:
-        copy.start()
-    for copy in copies:
-        copy.wait()
+    half = damage_ref.shape[0] // 2
+    for low in (0, half):
+        here = pl.ds(low, half)
+        for i in range(moved_ref.shape[0]):
+            pltpu.make_async_copy(moved_ref.at[i, here], moved_hbm.at[i, here], sem.at[0]).start()
+        pltpu.make_async_copy(damage_ref.at[here], damage_hbm.at[here], sem.at[1]).start()
+    last = pltpu.make_async_copy(read_ref, read_hbm, sem.at[2])
+    last.start()
+    pltpu.make_async_copy(moved_ref, moved_hbm, sem.at[0]).wait()
+    pltpu.make_async_copy(damage_ref, damage_hbm, sem.at[1]).wait()
+    last.wait()
 
 
 def solution(mesh):

time: 27.4 us -> 26.6 us (0.971)
  Pallas kernels: 26.6 us -> 25.8 us
    pallas_call x1, Pallas kernels: 25.6 us -> 24.8 us  [local(): pl.pallas_call(make_kernel(Z, R, C, S, sizes, first_slab, owners), out_sh...]
where the time goes in v4:
time: 26.6 us; the launch traced here: 26.4 us
  Pallas kernels  25.8 us (97%)
  between operations  0.64 us (2%)
    pallas_call x1, Pallas kernels, local(): pl.pallas_call(make_kernel(Z, R, C, S, sizes, first_slab, owners), out_sh...  24.8 us
    pallas_call x1, Pallas kernels, local(): pl.pallas_call(emit, out_shape=shapes, in_specs=[vmem_spec] * 3, out_spec...  1 us

profile of v4, /device:TPU:0, one launch (start us, length us, event | category | flops | bytes accessed | tf_op | source)
XLA Modules:
  0.0 26.4 jit_solution(7342417500300467139)
XLA Ops:
  0.6 24.8 %fracture.1 = (f32[3,8,32,256]{3,2,1,0:T(8,128)S(1)}, f32[8,32,256]{2,1,0:T(8,128)S(1)}, f32[3,4096]{1,0:T(4,128)S(1)}) custom-call(f32[3,8,32,256]{3,2,1,0:T(8,128)} %u_hbm.1, f32[8,32,256]{2,1,0:T(8,128)} %tough_hbm.1, s32[8,32,256]{2,1,0:T(8,128)} %crack_hbm.1, bf16[256,4096]{1,0:T(8,128)(2,1)} %bitcast.2, s32[1,4096]{1,0:T(1,128)} %bitcast.3), custom_call_target="tpu_custom_call" | custom-call | tf_op jit(solution)/shard_map/fracture/pallas_call | solution.py:950
  25.4 1.0 %emit.1 = (f32[3,8,32,256]{3,2,1,0:T(8,128)}, f32[8,32,256]{2,1,0:T(8,128)}, f32[3,4096]{1,0:T(4,128)}) custom-call(f32[3,8,32,256]{3,2,1,0:T(8,128)S(1)} %get-tuple-element.6.moved_ref, f32[8,32,256]{2,1,0:T(8,128)S(1)} %get-tuple-element.7.damage_ref, f32[3,4096]{1,0:T(4,128)S(1)} %get-tuple-element.8.read_ref), custom_call_target="tpu_custom_call" | custom-call | tf_op jit(solution)/shard_map/emit/pallas_call | solution.py:994

commit v5 on v4

--- a/solution.py
+++ b/solution.py
@@ -262,7 +262,7 @@
 
         def slot(step, kind):
             if step == 0:
-                return 0 if kind in EDGE else 1 if kind in REST else 2 if kind[0] == "x" else 3
+                return 11 if kind == "zu" else 0 if kind in EDGE else 1 if kind in REST else 2 if kind[0] == "x" else 3
             if kind[0] == "z":
                 return 4
             if kind[-1] == "0":
@@ -727,20 +727,21 @@
             loop(0, 2, lambda k: force_rim(0, 2 + k * (Z - 5), True))
             loop(0, 2, lambda k: force_rim(0, 1 + k * (Z - 3), True))
         with scope("waitza"):
-            receive(0, *EDGE)
+            receive(0, "zu")
         with scope("edge"):
             loop(0, 2, lambda k: ends(0, k * (Z - 1)))
             loop(0, 2, lambda k: finish(0, 1 + k * (Z - 3)))
         send(1, "zs")
-        unpack_zx(0)
-        for z in (-1, Z):
-            unpack_y(0, z, 3)
         with scope("body2"):
             loop(3, Z - 3, lambda z: force_rim(0, z, True))
             loop(2, Z - 2, lambda z: finish(0, z))
-            loop(0, 2, lambda k: force(0, k * (Z - 1)))
             pack_y(1, 0)
             send(1, "y0", "yx0", "x0")
+            receive(0, "zx", "zy")
+            unpack_zx(0)
+            for z in (-1, Z):
+                unpack_y(0, z, 3)
+            loop(0, 2, lambda k: force(0, k * (Z - 1)))
         with scope("waitzb"):
             receive(0, *REST)
         with scope("ends"):
@@ -976,7 +977,7 @@
                 pltpu.VMEM((owners, 3, piece // 128, 128), F32),
                 dma((6,)),
                 dma((3,)),
-                dma((11,)),
+                dma((12,)),
             ],
             compiler_params=pltpu.CompilerParams(
                 collective_id=0, has_side_effects=True, vmem_limit_bytes=40 * 1024 * 1024

time: 26.6 us -> 26.5 us (level)
  no operation moved by 1% of the time
where the time goes in v5:
time: 26.5 us; the launch traced here: 26.3 us
  Pallas kernels  25.7 us (97%)
  between operations  0.64 us (2%)
    pallas_call x1, Pallas kernels, local(): pl.pallas_call(make_kernel(Z, R, C, S, sizes, first_slab, owners), out_sh...  24.7 us
    pallas_call x1, Pallas kernels, local(): pl.pallas_call(emit, out_shape=shapes, in_specs=[vmem_spec] * 3, out_spec...  1 us

profile of v5, /device:TPU:0, one launch (start us, length us, event | category | flops | bytes accessed | tf_op | source)
XLA Modules:
  0.0 26.3 jit_solution(15487512572664726804)
XLA Ops:
  0.6 24.7 %fracture.1 = (f32[3,8,32,256]{3,2,1,0:T(8,128)S(1)}, f32[8,32,256]{2,1,0:T(8,128)S(1)}, f32[3,4096]{1,0:T(4,128)S(1)}) custom-call(f32[3,8,32,256]{3,2,1,0:T(8,128)} %u_hbm.1, f32[8,32,256]{2,1,0:T(8,128)} %tough_hbm.1, s32[8,32,256]{2,1,0:T(8,128)} %crack_hbm.1, bf16[256,4096]{1,0:T(8,128)(2,1)} %bitcast.2, s32[1,4096]{1,0:T(1,128)} %bitcast.3), custom_call_target="tpu_custom_call" | custom-call | tf_op jit(solution)/shard_map/fracture/pallas_call | solution.py:951
  25.3 1.0 %emit.1 = (f32[3,8,32,256]{3,2,1,0:T(8,128)}, f32[8,32,256]{2,1,0:T(8,128)}, f32[3,4096]{1,0:T(4,128)}) custom-call(f32[3,8,32,256]{3,2,1,0:T(8,128)S(1)} %get-tuple-element.6.moved_ref, f32[8,32,256]{2,1,0:T(8,128)S(1)} %get-tuple-element.7.damage_ref, f32[3,4096]{1,0:T(4,128)S(1)} %get-tuple-element.8.read_ref), custom_call_target="tpu_custom_call" | custom-call | tf_op jit(solution)/shard_map/emit/pallas_call | solution.py:995
